TPU v7x, 256 devices: a whole 4x4x8 slice. The times are simulated.
256 devices in a mesh: seq: 16 (over z, core), head: 16 (over x, y).
Axes of the slice: x: 4, y: 4, z: 8, core: 2. Of those that a mesh axis runs over, the one named last changes fastest.
Arguments:
- grad_output: bfloat16 [16384, 4096], P('seq', 'head'), may hold values from -6 to 6
- out_weight: bfloat16 [4096, 8192], P('seq', 'head'), may hold values from -0.0625 to 0.0625
- ssd_out: bfloat16 [16384, 8192], P('seq', 'head'), may hold values from -520 to 520
- gate: bfloat16 [16384, 8192], P('seq', 'head'), may hold values from -5 to 5
- norm_weight: float32 [8192], P('head'), may hold values from 0.5 to 1.5
- time_step: float32 [128, 16384], P('head', 'seq'), may hold values from 0.01 to 0.1
- log_decay: float32 [128, 16384], P('head', 'seq'), may hold values from -0.7 to 0
- state_in: bfloat16 [16384, 8, 128], P('seq'), may hold values from -1.796875 to 1.796875
- state_out: bfloat16 [16384, 8, 128], P('seq'), may hold values from -1.796875 to 1.796875
- skip: float32 [128], P('head'), may hold values from 0.5 to 1.5
Outputs:
- grad_x: bfloat16 [16384, 8192], P('seq', 'head')
- grad_gate: bfloat16 [16384, 8192], P('seq', 'head')
- grad_out_weight: float32 [4096, 8192], P('seq', 'head')
All inputs are finite; a program needn't handle non-finite values.
Results may differ from a plain program's by a relative error of at most 0.014.
Values may be sent and summed in bfloat16 or wider, within the bound.
A program may use at most 128 MiB of HBM per device.

v0:
```python
import math

import jax
import jax.numpy as jnp
from jax import lax
from jax.sharding import Mesh
from jax.sharding import PartitionSpec as P

HEADS = 128
GROUPS = 8
BLOCK_LEN = 256
HEAD = ("head_0", "head_1")
SEQ = ("seq_0", "seq_1")


epsilon = 1e-05


def over_axes(x, axes):
    for axis in axes:
        x = lax.psum(x, axis)
    return x


def nothing_yet(x, identity):
    return jax.tree.map(
        lambda part, zero: jnp.zeros_like(part) + jnp.asarray(zero, part.dtype), x, identity
    )


def carried_in(x, axes, combine, identity):
    before = start = nothing_yet(x, identity)
    running = x
    for axis in reversed(axes):
        size, here = (lax.axis_size(axis), lax.axis_index(axis))
        pieces = jax.tree.map(lambda part: lax.all_gather(part, axis), running)
        inside, running = (start, start)
        for k in reversed(range(size)):
            passed = k > here
            running = combine(running, jax.tree.map(lambda part: part[k], pieces))
            inside = jax.tree.map(lambda new, old: jnp.where(passed, new, old), running, inside)
        before = combine(inside, before)
    return before


def on_device(
    grad_output,
    out_weight,
    ssd_out,
    gate,
    norm_weight,
    time_step,
    log_decay,
    state_in,
    state_out,
    skip,
):
    tok_rows = ssd_out.shape[0]
    local_width = ssd_out.shape[1]
    total_width = local_width * lax.axis_size(HEAD)
    full_grad = lax.all_gather(grad_output, HEAD, axis=1, tiled=True)
    values = ssd_out.astype(jnp.float32)
    gate_values = gate.astype(jnp.float32)
    sigmoid_gate = jax.nn.sigmoid(gate_values)
    silu_gate = gate_values * sigmoid_gate
    gated_values = values * silu_gate
    local_squares = jnp.sum(gated_values * gated_values, axis=1)
    columns = full_grad
    normed_grad = jnp.dot(
        columns,
        lax.all_gather(out_weight, SEQ, axis=0, tiled=True),
        preferred_element_type=jnp.float32,
    )
    squares = over_axes(local_squares, HEAD)
    weighted = over_axes(jnp.sum(norm_weight * normed_grad * gated_values, axis=1), HEAD)
    inverse_rms = lax.rsqrt(squares[:, None] / total_width + epsilon)
    normed = (gated_values * inverse_rms * norm_weight).astype(jnp.bfloat16)
    gated_grad = (
        inverse_rms * norm_weight * normed_grad
        - gated_values * inverse_rms**3 * weighted[:, None] / total_width
    )
    grad_gate = (
        gated_grad * values * sigmoid_gate * (1.0 + gate_values * (1.0 - sigmoid_gate))
    ).astype(jnp.bfloat16)
    grad_ssd = (gated_grad * silu_gate).astype(jnp.bfloat16)
    columns = full_grad
    weight_sum = lax.psum_scatter(
        lax.dot_general(
            columns, normed, (((0,), (0,)), ((), ())), preferred_element_type=jnp.float32
        ).astype(jnp.bfloat16),
        SEQ,
        scatter_dimension=0,
        tiled=True,
    ).astype(jnp.float32)
    grad_out_weight = weight_sum * (1.0 / math.sqrt(tok_rows * lax.axis_size(SEQ)))
    heads_here = time_step.shape[0]
    head_width = local_width // heads_here
    blocks = tok_rows // BLOCK_LEN
    state_width = state_in.shape[2]
    group_count = state_in.shape[1]
    first_head = lax.axis_index(HEAD) * heads_here
    head_ids = first_head + jnp.arange(heads_here, dtype=jnp.int32)
    group_ids = head_ids // (HEADS // GROUPS)
    group_pick = (group_ids[:, None] == jnp.arange(group_count, dtype=jnp.int32)[None, :]).astype(
        jnp.bfloat16
    )
    b_heads = jnp.einsum(
        "tgn,hg->htn", state_in, group_pick, preferred_element_type=jnp.float32
    ).astype(jnp.bfloat16)
    b_heads = b_heads.reshape(heads_here, blocks, BLOCK_LEN, state_width)
    c_heads = jnp.einsum(
        "tgn,hg->htn", state_out, group_pick, preferred_element_type=jnp.float32
    ).astype(jnp.bfloat16)
    c_heads = c_heads.reshape(heads_here, blocks, BLOCK_LEN, state_width)
    grad_heads = grad_ssd.reshape(tok_rows, heads_here, head_width).transpose(1, 0, 2)
    grad_heads = grad_heads.reshape(heads_here, blocks, BLOCK_LEN, head_width)
    cumulative = jnp.cumsum(log_decay.reshape(heads_here, blocks, BLOCK_LEN), axis=2)
    block_total = cumulative[..., -1]
    sequence_indices = jnp.arange(BLOCK_LEN)
    upper_mask = sequence_indices[None, :] >= sequence_indices[:, None]
    scores = jnp.einsum("hktn,hksn->hkts", b_heads, c_heads, preferred_element_type=jnp.float32)
    log_gap = cumulative[..., None, :] - cumulative[..., :, None]
    block_weights = jnp.where(upper_mask, scores * jnp.exp(jnp.minimum(log_gap, 0.0)), 0.0).astype(
        jnp.bfloat16
    )
    within = jnp.einsum(
        "hkts,hksp->hktp", block_weights, grad_heads, preferred_element_type=jnp.float32
    )
    grad_float = grad_heads.astype(jnp.float32)
    scaled = (jnp.exp(cumulative)[..., None] * grad_float).astype(jnp.bfloat16)
    block_state = jnp.einsum("hksp,hksn->hkpn", scaled, c_heads, preferred_element_type=jnp.float32)

    def fold_block(carried, inputs):
        state_now, total_now = inputs
        return (state_now + jnp.exp(total_now)[:, None, None] * carried, carried)

    zero_state = jnp.zeros((heads_here, head_width, state_width), jnp.float32)
    summary, inside = lax.scan(
        fold_block, zero_state, (block_state.transpose(1, 0, 2, 3), block_total.T), reverse=True
    )
    decay_total = jnp.exp(jnp.sum(block_total, axis=1))
    tail_decay = jnp.exp(
        jnp.sum(block_total, axis=1, keepdims=True) - jnp.cumsum(block_total, axis=1)
    )

    def combine_pair(earlier, later):
        return (later[0] * earlier[0], later[1] + later[0][:, None, None] * earlier[1])

    identity = (jnp.ones((heads_here,), jnp.float32), zero_state)
    prefix = carried_in((decay_total, summary), SEQ, combine_pair, identity)
    remote = prefix[1]
    full_states = inside.transpose(1, 0, 2, 3) + tail_decay[..., None, None] * remote[:, None]
    carry_low = full_states.astype(jnp.bfloat16)
    across = jnp.einsum("hkpn,hktn->hktp", carry_low, b_heads, preferred_element_type=jnp.float32)
    across = across * jnp.exp(block_total[..., None] - cumulative)[..., None]
    step_sizes = time_step.reshape(heads_here, blocks, BLOCK_LEN)
    grad_head = step_sizes[..., None] * (within + across) + skip[:, None, None, None] * grad_float
    grad_x = (
        grad_head.reshape(heads_here, tok_rows, head_width)
        .transpose(1, 0, 2)
        .reshape(tok_rows, local_width)
    )
    return (grad_x.astype(jnp.bfloat16), grad_gate, grad_out_weight)


def solution(mesh):
    finer = Mesh(mesh.devices.reshape(8, 2, 4, 4), ("seq_0", "seq_1", "head_0", "head_1"))
    return jax.shard_map(
        on_device,
        mesh=finer,
        in_specs=(
            P(SEQ, HEAD),
            P(SEQ, HEAD),
            P(SEQ, HEAD),
            P(SEQ, HEAD),
            P(HEAD),
            P(HEAD, SEQ),
            P(HEAD, SEQ),
            P(SEQ, None, None),
            P(SEQ, None, None),
            P(HEAD),
        ),
        out_specs=(P(SEQ, HEAD), P(SEQ, HEAD), P(SEQ, HEAD)),
        check_vma=False,
    )
```

profile of v0, /device:TPU:21, one launch (start us, length us, event | category | flops | bytes accessed | tf_op | source)
XLA Modules:
  0.0 290.6 jit_solution(11251501523468864543)
XLA Ops:
  7.2 0.0 copy-start
  7.2 0.0 all-gather.9.cloned.1.call-start
  7.2 0.7 all-gather.9.cloned.1.call-update
  7.9 0.0 all-gather.7.cloned.1.call-start
  8.0 0.7 all-gather.7.cloned.1.call-update
  8.7 0.0 all-gather.11.cloned.1.call-start
  8.7 1.3 dynamic-slice.1
  10.0 1.3 dynamic-slice
  12.6 0.8 copy.70
  13.3 2.3 reduce-window.6
  15.6 0.2 slice_reduce_fusion
  15.8 0.1 copy_bitcast_fusion
  15.8 0.2 slice_reduce_fusion.1
  16.1 0.1 fusion.63
  16.2 1.5 copy.74
  17.7 0.0 copy-start.2
  17.7 2.6 copy.75
  20.3 0.1 exponential_dynamic-update-slice_fusion
  20.4 2.8 all-reduce
  23.2 0.2 broadcast_select_fusion.1
  23.4 0.0 copy-done
  23.4 2.1 convolution_convert_fusion.1
  25.5 0.0 copy-done.9
  25.5 29.3 %all-gather.9.cloned.1.call-done = bf16[4096,512]{1,0:T(8,128)(2,1)} async-done(((bf16[256,512]{1,0:T(8,128)(2,1)}), bf16[4096,512]{1,0:T(8,128)(2,1)}) %all-gather.9.cloned.1.call-update) | async-done | bytes 4194320 | tf_op jit(solution)/shard_map/all_gather | solution.py:71
  54.9 79.6 %all-gather.7.cloned.1.call-done = bf16[1024,4096]{1,0:T(8,128)(2,1)} async-done(((bf16[1024,256]{1,0:T(8,128)(2,1)}), bf16[1024,4096]{1,0:T(8,128)(2,1)}) %all-gather.7.cloned.1.call-update) | async-done | bytes 8388624 | tf_op jit(solution)/shard_map/all_gather | solution.py:61
  134.4 0.0 copy-done.7
  134.4 11.3 %multiply_reduce_fusion.1 = (f32[1024]{0:T(1024)S(1)}, f32[1024]{0:T(1024)S(1)}, f32[1024,512]{0,1:T(8,128)}) fusion(bf16[1024,512]{0,1:T(8,128)(2,1)S(1)} %copy.74, bf16[1024,512]{0,1:T(8,128)(2,1)} %copy.75, f32[512]{0:T(512)S(1)} %copy-done.7, bf16[1024,4096]{1,0:T(8,128)(2,1)} %all-gather.7.cloned.1.call-done, ...), kind=kOutput, calls=%fused_computation.32 | convolution fusion | flops 4301256704 | bytes 16787456 | tf_op jit(solution)/shard_map/dot_general | solution.py:69
  145.7 6.7 %all-reduce.3 = (f32[1024]{0:T(1024)S(1)}, f32[1024]{0:T(1024)S(1)}) all-reduce(f32[1024]{0:T(1024)S(1)} %get-tuple-element.160, f32[1024]{0:T(1024)S(1)} %get-tuple-element.159), channel_id=1, replica_groups=mesh['seq_0'=8,'seq_1'=2,'head_0'=4,'head_1'=4] {'head_0'}, use_global_device_ids=true, to_apply=%region_6.0 | all-reduce | flops 2048 | bytes 16384 | tf_op jit(solution)/shard_map/psum | solution.py:21
  152.4 5.8 %all-reduce.2 = (f32[1024]{0:T(1024)S(1)}, f32[1024]{0:T(1024)S(1)}) all-reduce(f32[1024]{0:T(1024)S(1)} %get-tuple-element.175, f32[1024]{0:T(1024)S(1)} %get-tuple-element.176), channel_id=1, replica_groups=mesh['seq_0'=8,'seq_1'=2,'head_0'=4,'head_1'=4] {'head_1'}, use_global_device_ids=true, to_apply=%region_7.8 | all-reduce | flops 2048 | bytes 16384 | tf_op jit(solution)/shard_map/psum | solution.py:21
  158.2 0.0 copy-done.2
  158.2 0.0 copy-start.5
  158.2 4.7 %fusion.9 = (bf16[1024,512]{0,1:T(8,128)(2,1)}, bf16[1024,512]{0,1:T(8,128)(2,1)S(1)}) fusion(bf16[1024,512]{0,1:T(8,128)(2,1)S(1)} %copy.74, bf16[1024,512]{0,1:T(8,128)(2,1)} %copy.75, f32[1024]{0:T(1024)S(1)} %get-tuple-element.173, f32[1024]{0:T(1024)S(1)} %get-tuple-element.182, f32[1024,512]{0,1:T(8,128)} %get-tuple-element.195, f32[512]{0:T(512)S(1)} %copy-done.7, ...), kind=kLoop, calls=%fused_computation.20 | loop fusion | flops 11534336 | bytes 6305792 | tf_op jit(solution)/shard_map/convert_element_type | solution.py:84
  162.9 0.0 copy-done.5
  162.9 1.8 fusion.27
  164.7 0.0 copy-done.3
  164.7 0.1 broadcast_in_dim.27
  164.8 4.5 %while.17 = (s32[]{:T(128)}, f32[8,64,128]{2,1,0:T(8,128)S(1)}, f32[4,8,64,128]{3,2,1,0:T(8,128)S(1)}, f32[4,8,64,128]{3,2,0,1:T(8,128)}, f32[4,8]{1,0:T(4,128)S(1)}, /*index=5*/s32[]{:T(128)}, s32[]{:T(128)}, s32[]{:T(128)}) while((s32[]{:T(128)}, f32[8,64,128]{2,1,0:T(8,128)S(1)}, f32[4,8,64,128]{3,2,1,0:T(8,128)S(1)}, ...), condition=%wide.region_9.10_spmd.clone, body=%wide.region_8.9_spmd.clone.sunk | while | flops 262148 | bytes 1310944 | solution.py:138
  164.8 1.1 bitcast_add_fusion.4
  166.0 1.1 bitcast_add_fusion.4
  167.1 1.1 bitcast_add_fusion.4
  168.2 1.1 bitcast_add_fusion.4
  169.3 0.0 copy-start.4
  169.3 1.0 copy-done.4
  170.3 7.8 %all-gather = f32[16,64,128]{2,1,0:T(8,128)S(1)} all-gather(f32[8,64,128]{2,1,0:T(8,128)S(1)} %get-tuple-element.108), channel_id=2, replica_groups=mesh['seq_0'=8,'seq_1'=2,'head_0'=4,'head_1'=4] {'seq_1'}, dimensions={0}, use_global_device_ids=true | all-gather | bytes 786432 | tf_op jit(solution)/shard_map/all_gather | solution.py:36
  178.1 0.8 fusion.55
  178.9 0.0 all-gather.11.cloned.1.call-update
  178.9 0.2 reduce-scatter.2.cloned.1.call-start
  179.2 11.0 %fusion.2 = bf16[4096,512]{0,1:T(8,128)(2,1)} fusion(bf16[1024,4096]{1,0:T(8,128)(2,1)} %all-gather.7.cloned.1.call-done, f32[512]{0:T(512)S(1)} %copy-done.7, bf16[1024,512]{0,1:T(8,128)(2,1)} %copy-done.2, f32[1024]{0:T(1024)S(1)} %get-tuple-element.181, bf16[1024,512]{0,1:T(8,128)(2,1)} %copy.75), kind=kOutput, calls=%fused_computation.7 | convolution fusion | flops 4302307328 | bytes 14686208 | tf_op jit(solution)/shard_map/dot_general | solution.py:88
  190.2 0.0 reduce-scatter.2.cloned.1.call-update
  190.3 0.7 copy-done.6
  191.0 0.0 copy-done.10
  191.0 14.9 %all-reduce.1 = f32[64]{0:T(128)S(1)} all-reduce(f32[64]{0:T(128)S(1)} %copy-done.10), channel_id=4, replica_groups=mesh['seq_0'=8,'seq_1'=2,'head_0'=4,'head_1'=4] {'seq_0'}, use_global_device_ids=true, to_apply=%add.1 | all-reduce | flops 64 | bytes 512
  205.9 0.1 fusion.64
  206.0 3.7 %convolution_convert_fusion.2 = bf16[8,1024,128]{2,0,1:T(8,128)(2,1)} fusion(bf16[1024,8,128]{2,1,0:T(8,128)(2,1)} %param.19, s32[8]{0:T(128)S(1)} %and_select_fusion), kind=kOutput, calls=%fused_computation.34 | convolution fusion | flops 17825856 | bytes 4194336 | tf_op jit(solution)/shard_map/tgn,hg->htn/dot_general | solution.py:107
  209.7 2.3 copy.86
  211.9 6.4 %fusion.3 = f32[8,4,256,64]{2,3,1,0:T(8,128)} fusion(f32[8,4,256]{2,1,0:T(4,128)S(1)} %copy.72, pred[256,256]{1,0:T(8,128)(4,1)S(1)} %iota_compare_fusion, bf16[8,4,256,128]{3,0,2,1:T(8,128)(2,1)} %bitcast.136, bf16[8,4,256,128]{3,0,2,1:T(8,128)(2,1)} %bitcast.130, bf16[8,8,4,8,256]{4,3,2,1,0:T(8,128)(2,1)} %bitcast.133), kind=kOutput, calls=%fused_computation.8 | convolution fusion | flops 815792128 | bytes 7438336 | tf_op jit(solution)/shard_map/hkts,hksp->hktp/dot_general | solution.py:126
  218.3 2.1 fusion.53
  220.4 0.1 copy-done.1
  220.5 3.3 %fusion.30 = bf16[8,4,8,8,256]{4,3,2,1,0:T(8,128)(2,1)S(1)} fusion(f32[8,4,256,64]{2,3,1,0:T(8,128)} %fusion.3, bf16[8,4,256,128]{3,0,2,1:T(8,128)(2,1)S(1)} %bitcast.131, f32[8]{0:T(128)S(1)} %copy-done.8, f32[8,4,256]{2,1,0:T(4,128)S(1)} %copy.83, f32[8,4,256]{2,1,0:T(4,128)S(1)} %copy.67, bf16[8,8,4,8,256]{4,3,2,1,0:T(8,128)(2,1)} %bitcast.134, ...), kind=kOutput, calls=%fused_computation.42 | convolution fusion | flops 138674176 | bytes 7667872 | tf_op jit(solution)/shard_map/hkpn,hktn->hktp/dot_general | solution.py:154
  223.8 0.1 copy.91
  224.0 1.3 copy.85
  225.3 56.8 %reduce-scatter.2.cloned.1.call-done = bf16[256,512]{0,1:T(8,128)(2,1)} async-done(((bf16[4096,512]{0,1:T(8,128)(2,1)}), bf16[256,512]{0,1:T(8,128)(2,1)}) %reduce-scatter.2.cloned.1.call-update) | async-done | bytes 262160 | tf_op jit(solution)/shard_map/reduce_scatter | solution.py:87
  282.1 1.0 convert_multiply_fusion.7
  283.1 1.0 copy.87
  (31 shorter events, 0.3 us)
Async XLA Ops:
  7.2 16.2 %copy-start = (bf16[1024,8,128]{2,1,0:T(8,128)(2,1)S(1)}, bf16[1024,8,128]{2,1,0:T(8,128)(2,1)}, u32[]{:S(2)}) copy-start(bf16[1024,8,128]{2,1,0:T(8,128)(2,1)} %param.20) | copy-start | bytes 6291460
  7.2 47.7 %all-gather.9.cloned.1.call-start = ((), (), s32[]{:S(2)}) async-start(), calls=%async_computation.2 | async-start | bytes 4456448 | tf_op jit(solution)/shard_map/all_gather | solution.py:71
  7.9 126.5 %all-gather.7.cloned.1.call-start = ((), (), s32[]{:S(2)}) async-start(), calls=%async_computation.1 | async-start | bytes 8912896 | tf_op jit(solution)/shard_map/all_gather | solution.py:61
  8.7 209.6 %all-gather.11.cloned.1.call-start = ((), (), s32[]{:S(2)}) async-start(), calls=%async_computation.3 | async-start | bytes 2359296 | tf_op jit(solution)/shard_map/all_gather | solution.py:36
  17.7 140.5 %copy-start.2 = (bf16[1024,512]{0,1:T(8,128)(2,1)}, bf16[1024,512]{0,1:T(8,128)(2,1)S(1)}, u32[]{:S(2)}) copy-start(bf16[1024,512]{0,1:T(8,128)(2,1)S(1)} %copy.74) | copy-start | bytes 3145732
  23.4 2.1 copy-start.9
  23.4 111.0 %copy-start.7 = (f32[512]{0:T(512)S(1)}, f32[512]{0:T(512)}, u32[]{:S(2)}) copy-start(f32[512]{0:T(512)} %param.16) | copy-start | bytes 6148
  158.2 4.7 %copy-start.5 = (bf16[8,1024,128]{2,0,1:T(8,128)(2,1)S(1)}, bf16[8,1024,128]{2,0,1:T(8,128)(2,1)}, u32[]{:S(2)}) copy-start(bf16[8,1024,128]{2,0,1:T(8,128)(2,1)} %convolution_convert_fusion.1) | copy-start | bytes 6291460
  162.9 1.8 copy-start.3
  169.3 1.0 copy-start.4
  178.9 103.1 %reduce-scatter.2.cloned.1.call-start = ((), (), s32[]{:S(2)}) async-start(), calls=%async_computation.4 | async-start | bytes 4456448 | tf_op jit(solution)/shard_map/reduce_scatter | solution.py:87
  190.2 0.8 copy-start.6
  190.2 0.8 copy-start.10
  218.3 2.1 copy-start.8
  218.3 2.2 copy-start.1
Sparse Core Ops, SparseCore 0:
  9.8 45.0 all-gather.8
  57.3 77.1 all-gather.6
  179.1 37.9 all-gather.10
  219.5 62.5 reduce-scatter.1
where the time goes:
time: 295 us; the launch traced here: 291 us
  waiting for transfers between devices  167 us (57%)
  matrix products  39.5 us (13%)
  blocking collectives  38 us (13%)
  other arithmetic  15.8 us (5%)
  between operations  15.3 us (5%)
  local copies, waits for them, and re-layouts  14.4 us (5%)
    all_gather x1, waiting for transfers between devices, on_device(): full_grad = lax.all_gather(grad_output, HEAD, axis=1, tiled=True)  79.6 us
    reduce_scatter x1, waiting for transfers between devices, on_device(): lax.psum_scatter(lax.dot_general(columns, normed, (((0,), (0,)), ((), ())...  56.8 us
    all_gather x1, waiting for transfers between devices, on_device(): lax.all_gather(out_weight, SEQ, axis=0, tiled=True)  29.3 us
    unnamed x2, blocking collectives  17.7 us
    unnamed x32, local copies, waits for them, and re-layouts  13.2 us
    psum x2, blocking collectives, over_axes(): x = lax.psum(x, axis)  12.5 us
    dot_general x1, matrix products, on_device(): jnp.dot(columns, lax.all_gather(out_weight, SEQ, axis=0, tiled=True), pre...  11.3 us
    dot_general x1, matrix products, on_device(): lax.dot_general(columns, normed, (((0,), (0,)), ((), ())), preferred_elem...  11 us
  transfers between devices with their start and end apart: 4, of which 3 were waited for; matrix products, arithmetic and copies ran while one was open for 15% of the time, Pallas kernels for 0%

commit v1 on v0

v1 whole, which is shorter than its diff:
```python
import functools
import math

import jax
import jax.numpy as jnp
from jax import lax
from jax.experimental import pallas as pl
from jax.experimental.pallas import tpu as pltpu
from jax.sharding import Mesh
from jax.sharding import PartitionSpec as P

EPS = 1e-05
F32, BF16 = jnp.float32, jnp.bfloat16
MESH = pl.DeviceIdType.MESH
BLK = 256
A, B = (0, 512), (512, 512)
A0, A1, B0, B1 = (0, 256), (256, 256), (512, 256), (768, 256)
STEP = ((1, 0), (-1, 0), (0, 1), (0, -1))
ITEMS = (
    ((0, 0, A), (0, 0, B), (-1, 0, A), (0, 1, B), (0, -1, B), (0, 2, B), (-1, 1, B0), (-1, -1, B0), (-1, 2, B0)),
    ((0, 0, A), (0, 0, B), (1, 0, B), (0, 1, B), (0, -1, B), (0, 2, B), (1, 1, B1), (1, -1, B1), (1, 2, B1)),
    ((0, 0, B), (0, 0, A), (0, -1, A), (1, 0, A), (-1, 0, A), (2, 0, A), (1, -1, A0), (-1, -1, A0), (2, -1, A0)),
    ((0, 0, B), (0, 0, A), (0, 1, B), (1, 0, A), (-1, 0, A), (2, 0, A), (1, 1, A1), (-1, 1, A1), (2, 1, A1)),
)
PAIRS = (
    ((0, 0), (0, 1)),
    ((1, 0), (0, -1)),
    ((-1, 0), (1, 1)),
    ((2, 0), (-1, 1)),
    ((0, 2), (1, -1)),
    ((1, 2), (-1, -1)),
    ((-1, 2), (2, 1)),
    ((2, 2), (2, -1)),
)
ECUM, ETAIL, TSTEP, CUM = 0, 24, 48, 72


def split3(q):
    first = q.astype(BF16).astype(F32)
    second = (q - first).astype(BF16).astype(F32)
    third = (q - first - second).astype(BF16).astype(F32)
    return [first, second, third]


def fold_lanes(v):
    return (v[:, 0:128] + v[:, 128:256]) + (v[:, 256:384] + v[:, 384:512])


def kernel(
    a_hbm, w_hbm, so_hbm, gt_hbm, nw_ref, ts_ref, ld_ref, bin_hbm, cin_hbm, skip_ref,
    gx_hbm, gg_hbm, gw_hbm,
    abuf, wbuf, so, gt, gated, silu, fgate, ng, ecw, etw, tsw, wts, gkeep, gout, gin, fromr, froml,
    normt, stage, conv, bsel, csel, ct, qt, cum_s, col, sqs, wds, st, schip, s0buf, d0buf, carry, msend, csend, gw,
    a_ssem, a_rsem, w_ssem, w_rsem, b_ssem, b_rsem, r_ssem, r_rsem, g_ssem, g_rsem, h_ssem, h_rsem,
    d_ssem, d_rsem, s_ssem, s_rsem, c_ssem, c_rsem, m_ssem, l_sem,
):
    z, c, x, y = (lax.axis_index(n) for n in ("z", "c", "x", "y"))
    head = x * 4 + y

    def at(dz=0, dc=0, dx=0, dy=0):
        return ((z + dz + 8) % 8, (c + dc) % 2, (x + dx + 4) % 4, (y + dy + 4) % 4)

    def slot(dx, dy):
        return ((x + dx + 4) % 4) * 4 + (y + dy + 4) % 4

    def remote(src, dst, ssem, rsem, dev):
        return pltpu.make_async_remote_copy(
            src_ref=src, dst_ref=dst, send_sem=ssem, recv_sem=rsem, device_id=dev, device_id_type=MESH
        )

    loads = [
        pltpu.make_async_copy(a_hbm, abuf.at[head], l_sem.at[0]),
        pltpu.make_async_copy(w_hbm, wbuf.at[z * 2 + c], l_sem.at[1]),
        pltpu.make_async_copy(so_hbm, so, l_sem.at[2]),
        pltpu.make_async_copy(gt_hbm, gt, l_sem.at[3]),
        pltpu.make_async_copy(bin_hbm, stage.at[0], l_sem.at[4]),
        pltpu.make_async_copy(cin_hbm, stage.at[1], l_sem.at[5]),
    ]
    for load in loads:
        load.start()
    barrier = pltpu.get_barrier_semaphore()

    def greet(k, carry_):
        other = (head + k) % 16
        pl.semaphore_signal(barrier, inc=1, device_id=(z, c, other // 4, other % 4), device_id_type=MESH)
        return carry_

    lax.fori_loop(1, 16, greet, 0)
    for dev in (at(dz=1), at(dz=-1), at(dc=1)):
        pl.semaphore_signal(barrier, inc=1, device_id=dev, device_id_type=MESH)
    loads[0].wait()
    loads[1].wait()
    pl.semaphore_wait(barrier, 18)

    def a_copy(d, k, got):
        dx, dy, (row, n) = ITEMS[d][k]
        sx, sy = STEP[d]
        here = slot(dx - sx, dy - sy) if got else slot(dx, dy)
        piece = abuf.at[here, pl.ds(row, n)]
        return remote(piece, piece, a_ssem.at[d, k], a_rsem.at[d, k], at(dx=sx, dy=sy))

    def a_send(*flows):
        for d, k in flows:
            a_copy(d, k, False).start()

    def a_wait(*flows):
        for d, k in flows:
            a_copy(d, k, True).wait_recv()

    every = lambda k: [(d, k) for d in range(4)]

    def w_copy(d, k, got):
        sign = 1 if d == 0 else -1
        far = (k // 2 if k < 6 else 3) + (1 if got else 0)
        half = k % 2 if k < 6 else d
        here = ((z - sign * far + 8) % 8) * 2 + c
        piece = wbuf.at[here, pl.ds(half * 128, 128)]
        return remote(piece, piece, w_ssem.at[d, k], w_rsem.at[d, k], at(dz=sign))

    def b_copy(k, got):
        here = ((z + k) % 8) * 2 + ((c + 1) % 2 if got else c)
        return remote(wbuf.at[here], wbuf.at[here], b_ssem.at[k], b_rsem.at[k], at(dc=1))

    def w_event(k):
        for d in (0, 1):
            w_copy(d, k, True).wait_recv()
            if k < 4:
                w_copy(d, k + 2, False).start()
        if k == 4:
            w_copy(0, 6, False).start()
        if k == 5:
            w_copy(1, 6, False).start()
        if k in (1, 3, 5):
            b_copy((k + 1) // 2, False).start()
            b_copy(8 - (k + 1) // 2, False).start()
        if k == 6:
            b_copy(4, False).start()

    a_send(*every(0), *every(1))
    for k in (0, 1):
        for d in (0, 1):
            w_copy(d, k, False).start()
    b_copy(0, False).start()

    def row_copy(slots, ssem, rsem, k, got):
        other = (head + k) % 16
        source = (head + 16 - k) % 16
        here = source if got else head
        return remote(slots.at[here], slots.at[here], ssem.at[k], rsem.at[k], (z, c, other // 4, other % 4))

    def row_send(slots, ssem, rsem):
        def one(k, carry_):
            row_copy(slots, ssem, rsem, k, False).start()
            return carry_

        lax.fori_loop(1, 16, one, 0)

    def row_sum(slots, ssem, rsem):
        def one(k, carry_):
            copy = row_copy(slots, ssem, rsem, k, True)
            copy.wait_recv()
            return carry_

        lax.fori_loop(1, 16, one, 0)
        total = slots[0]
        for k in range(1, 16):
            total = total + slots[k]
        return total

    def row_done(slots, ssem, rsem):
        def one(k, carry_):
            row_copy(slots, ssem, rsem, k, False).wait_send()
            return carry_

        lax.fori_loop(1, 16, one, 0)

    def to_column(row):
        return jnp.broadcast_to(row, (128, row.shape[1])).T

    def rows128(r):
        return pl.ds(pl.multiple_of(r * 128, 128), 128)

    loads[2].wait()
    loads[3].wait()

    @pl.loop(0, 8)
    def _(r):
        rows = rows128(r)
        values = so[rows, :].astype(F32)
        gate_values = gt[rows, :].astype(F32)
        sig = jax.nn.sigmoid(gate_values)
        sl = gate_values * sig
        gv = values * sl
        gated[rows, :] = gv
        silu[rows, :] = sl
        fgate[rows, :] = values * sig * (1.0 + gate_values * (1.0 - sig))
        sqs[head, :, rows] = jnp.sum(fold_lanes(gv * gv).T, axis=0, keepdims=True)

    row_send(sqs, g_ssem, g_rsem)
    w_event(0)

    rows_i = lax.broadcasted_iota(jnp.int32, (BLK, BLK), 0)
    cols_i = lax.broadcasted_iota(jnp.int32, (BLK, BLK), 1)
    tri = (rows_i <= cols_i).astype(F32).astype(BF16)
    for k in range(4):
        cols = slice(k * BLK, (k + 1) * BLK)
        parts = jnp.concatenate(split3(ld_ref[:, cols]), axis=0).astype(BF16)
        summed = jnp.dot(parts, tri, preferred_element_type=F32)
        cum = summed[0:8] + summed[8:16] + summed[16:24]
        cum_s[:, cols] = cum
        total = cum[:, BLK - 1 : BLK]
        table = (
            split3(jnp.exp(cum))
            + split3(jnp.exp(total - cum))
            + split3(ts_ref[:, cols])
            + [cum, jnp.zeros((128 - CUM - 8, BLK), F32)]
        )
        qt[cols, :] = jnp.concatenate(table, axis=0).T
    lane_head = lax.broadcasted_iota(jnp.int32, (128, 512), 1) // 64
    part_row = lax.broadcasted_iota(jnp.int32, (128, 512), 0)

    def pick(first):
        inside = (part_row >= first) & (part_row < first + 24) & ((part_row - first) % 8 == lane_head)
        return inside.astype(F32).astype(BF16)

    for first, wide in ((ECUM, ecw), (ETAIL, etw), (TSTEP, tsw)):
        chosen = pick(first)

        @pl.loop(0, 4)
        def _(k, chosen=chosen, wide=wide):
            rows = pl.ds(pl.multiple_of(k * BLK, BLK), BLK)
            wide[rows, :] = jnp.dot(qt[rows, :].astype(BF16), chosen, preferred_element_type=F32)

    decay_all = ecw[255:256, :] * ecw[511:512, :] * ecw[767:768, :] * ecw[1023:1024, :]
    d0buf[0] = decay_all

    a_wait(*every(0))
    a_send((0, 2), (0, 3), (0, 4), (1, 3), (3, 2), (3, 3), (3, 4), (2, 3))
    w_event(1)

    group = head // 2
    for which, (load, sel) in enumerate(((loads[4], bsel), (loads[5], csel))):
        load.wait()

        @pl.loop(0, 4)
        def _(r, which=which, sel=sel):
            conv[...] = stage[which, pl.ds(pl.multiple_of(r * 2048, 2048), 2048), :].astype(F32)
            sel[pl.ds(pl.multiple_of(r * 256, 256), 256), :] = conv[pl.ds(group, 256, stride=8), :].astype(BF16)

    mean = row_sum(sqs, g_ssem, g_rsem) * (1.0 / 8192)
    col[...] = to_column(lax.rsqrt(mean + EPS))
    w_event(2)
    nw = nw_ref[...]

    @pl.loop(0, 8)
    def _(r):
        rows = rows128(r)
        inv = col[rows, :][:, 0:1]
        normed = gated[rows, :] * inv * nw
        normt[:, rows] = normed.T.astype(BF16)

    ct[...] = csel[...].astype(F32).T.astype(BF16)

    a_wait(*every(1))
    a_send((1, 2), (1, 4), (2, 2), (2, 4))
    w_event(3)

    def pair_slots(p):
        (ex, ey), (ox, oy) = PAIRS[p]
        return slot(ex, ey), slot(ox, oy)

    def give_copy(p):
        return remote(gout.at[p], gin.at[p], h_ssem.at[p], h_rsem.at[p], at(dc=1))

    def weight_part(p):
        first, second = pair_slots(p)
        swap = (y + PAIRS[p][0][1] + 4 + c) % 2
        mine = jnp.where(swap == 0, first, second)
        other = jnp.where(swap == 0, second, first)

        @pl.loop(0, 4)
        def _(r):
            rows = rows128(r)
            lhs = normt[rows, :]
            gout[p, rows, :] = jnp.dot(lhs, abuf[other], preferred_element_type=F32).astype(BF16)
            gkeep[p, rows, :] = jnp.dot(lhs, abuf[mine], preferred_element_type=F32).astype(BF16)

        give_copy(p).start()

    def grad_part(p):
        first, second = pair_slots(p)

        @pl.loop(0, 4)
        def _(r):
            rows = pl.ds(pl.multiple_of(r * 256, 256), 256)
            add = jnp.dot(abuf[first, rows, :], wbuf[first], preferred_element_type=F32)
            add = add + jnp.dot(abuf[second, rows, :], wbuf[second], preferred_element_type=F32)
            if p == 0:
                ng[rows, :] = add
            else:
                ng[rows, :] += add

    def root_of(p):
        first, second = pair_slots(p)
        swap = (y + PAIRS[p][0][1] + 4 + c) % 2
        return jnp.where(swap == 0, first, second) // 2

    roots = [root_of(p) for p in range(8)]

    def tab(p):
        found = roots[0]
        for q in range(1, 8):
            found = jnp.where(p == q, roots[q], found)
        return found

    def r_copy(p, i, rightward, right_buf):
        piece = pl.ds(i * 256, 256)
        dev = ((z + jnp.where(rightward, 1, 7)) % 8, c, x, y)
        buf = fromr if right_buf else froml
        return remote(
            gkeep.at[p, piece], buf.at[p, piece], r_ssem.at[p, i], r_rsem.at[p, i, 0 if right_buf else 1], dev
        )

    def combine(p):
        give_copy(p).wait_recv()
        gkeep[p] = (gkeep[p].astype(F32) + gin[p].astype(F32)).astype(BF16)

    def rs_level(p, lev):
        rel = (z - tab(p) + 8) % 8
        for i in (0, 1):
            piece = pl.ds(i * 256, 256)
            rightward = rel >= 4 + i
            level = jnp.where(rightward, rel - (4 + i), (3 + i) - rel)

            def hop(right_buf, p=p, i=i, piece=piece):
                copy = r_copy(p, i, right_buf, right_buf)

                @pl.when(lev > 0)
                def _():
                    copy.wait_recv()
                    buf = fromr if right_buf else froml
                    gkeep[p, piece, :] = (gkeep[p, piece, :].astype(F32) + buf[p, piece, :].astype(F32)).astype(BF16)

                copy.start()

            live = (rel != 0) & (level == lev)

            @pl.when(live & rightward)
            def _():
                hop(True)

            @pl.when(live & jnp.logical_not(rightward))
            def _():
                hop(False)

        @pl.when((rel == 0) & (lev == 4))
        def _():
            for i in (0, 1):
                piece = pl.ds(i * 256, 256)
                r_copy(p, i, True, True).wait_recv()
                r_copy(p, i, False, False).wait_recv()
                gw[piece, :] = (
                    gkeep[p, piece, :].astype(F32) + fromr[p, piece, :].astype(F32) + froml[p, piece, :].astype(F32)
                ) * (1.0 / math.sqrt(16384.0))

    def rs_stage(t):
        if 0 < t <= 8:
            combine(t - 1)

        def one(lev, carry_):
            p = t - 1 - lev

            @pl.when((p >= 0) & (p < 8))
            def _():
                rs_level(p, lev)

            return carry_

        lax.fori_loop(0, 5, one, 0)

    def r_done():
        def one(p, carry_):
            rel = (z - tab(p) + 8) % 8

            @pl.when(rel != 0)
            def _():
                for i in (0, 1):
                    r_copy(p, i, True, True).wait_send()

            give_copy(p).wait_send()
            return carry_

        lax.fori_loop(0, 8, one, 0)

    weight_part(0)
    w_event(4)
    weight_part(1)
    a_wait((0, 2), (3, 2), (1, 3), (2, 3))
    a_send(*every(5))
    w_event(5)
    rs_stage(1)

    keep_upper = cols_i >= rows_i

    @pl.loop(0, 4)
    def _(k):
        rows = pl.ds(pl.multiple_of(k * BLK, BLK), BLK)
        scores = lax.dot_general(bsel[rows, :], csel[rows, :], (((1,), (1,)), ((), ())), preferred_element_type=F32)
        columns = qt[rows, :]
        for h in range(8):
            gap = cum_s[h : h + 1, rows] - columns[:, CUM + h : CUM + h + 1]
            weight = jnp.where(keep_upper, scores * jnp.exp(jnp.minimum(gap, 0.0)), 0.0)
            wts[k, h] = weight.astype(BF16)

    w_event(6)
    a_wait((0, 3), (1, 2), (2, 2), (3, 3))
    a_send(*every(6))
    weight_part(2)
    rs_stage(2)
    for k in range(8):
        b_copy(k, True).wait_recv()
    grad_part(0)
    grad_part(1)
    grad_part(2)
    a_wait(*every(4))
    a_send(*every(7))
    weight_part(3)
    rs_stage(3)
    grad_part(3)
    weight_part(4)
    rs_stage(4)
    a_wait(*every(5))
    a_send(*every(8))
    grad_part(4)
    a_wait(*every(6))
    weight_part(5)
    grad_part(5)
    a_wait(*every(7))
    weight_part(6)
    rs_stage(5)
    grad_part(6)
    a_wait(*every(8))
    grad_part(7)

    @pl.loop(0, 8)
    def _(r):
        rows = rows128(r)
        term = nw_ref[...] * ng[rows, :] * gated[rows, :]
        wds[head, :, rows] = jnp.sum(fold_lanes(term).T, axis=0, keepdims=True)

    row_send(wds, d_ssem, d_rsem)
    weight_part(7)
    rs_stage(6)
    weighted = row_sum(wds, d_ssem, d_rsem)

    cube = to_column(weighted * (1.0 / 8192))

    gs = gt

    for r in range(8):
        rows = slice(r * 128, (r + 1) * 128)
        inv = col[rows, 0:1]
        wcol = cube[rows, 0:1]
        gg = inv * nw_ref[...] * ng[rows, :] - gated[rows, :] * (inv * inv * inv * wcol)
        so[rows, :] = (gg * fgate[rows, :]).astype(BF16)
        gs[rows, :] = (gg * silu[rows, :]).astype(BF16)
    gate_out = pltpu.make_async_copy(so, gg_hbm, l_sem.at[0])
    gate_out.start()

    @pl.loop(0, 4)
    def _(k):
        rows = pl.ds(pl.multiple_of(k * BLK, BLK), BLK)
        scaled = (ecw[rows, :] * gs[rows, :].astype(F32)).astype(BF16)
        st[k] = jnp.dot(ct[:, rows], scaled, preferred_element_type=F32)

    ends = [ecw[k * BLK + BLK - 1 : k * BLK + BLK, :] for k in range(4)]

    def summary():
        return st[0] + ends[0] * (st[1] + ends[1] * (st[2] + ends[2] * st[3]))

    def s0_copy():
        return remote(msend, s0buf, s_ssem.at[0], s_rsem.at[0], (z, 1, x, y))

    def d0_copy():
        return remote(d0buf.at[0], d0buf.at[1], s_ssem.at[1], s_rsem.at[1], (z, 1, x, y))

    def chain_copy(q):
        piece = pl.ds(q * 32, 32)
        return remote(msend.at[piece], carry.at[piece], m_ssem.at[q], c_rsem.at[q], ((z + 7) % 8, 1, x, y))

    def core_copy(q):
        piece = pl.ds(q * 32, 32)
        return remote(csend.at[piece], carry.at[piece], c_ssem.at[q], c_rsem.at[q], (z, 0, x, y))

    @pl.when(c == 0)
    def _():
        msend[...] = summary().astype(BF16)
        d0_copy().start()
        s0_copy().start()

    @pl.when(c == 1)
    def _():
        schip[...] = summary()

    def within_all():
        low = lax.broadcasted_iota(jnp.int32, (BLK, 128), 1) < 64

        @pl.loop(0, 4)
        def _(k):
            rows = pl.ds(pl.multiple_of(k * BLK, BLK), BLK)
            for hp in range(4):
                cols = slice(hp * 128, hp * 128 + 128)
                g = gs[rows, cols]
                zero = jnp.zeros_like(g)
                ng[rows, cols] = jnp.dot(
                    wts[k, 2 * hp], jnp.where(low, g, zero), preferred_element_type=F32
                ) + jnp.dot(wts[k, 2 * hp + 1], jnp.where(low, zero, g), preferred_element_type=F32)

    def drain():
        for t in range(7, 13):
            rs_stage(t)

    ahead = (z >= 6) & (c == 1)

    @pl.when(jnp.logical_not(ahead))
    def _():
        within_all()

    @pl.when(c == 1)
    def _():
        d0_copy().wait_recv()
        s0_copy().wait_recv()
        d0 = d0buf[1]
        d1 = d0buf[0]
        for q in range(4):
            piece = pl.ds(q * 32, 32)

            @pl.when(z < 7)
            def _():
                chain_copy(q).wait_recv()

            @pl.when(z == 7)
            def _():
                carry[piece, :] = jnp.zeros((32, 512), BF16)

            own = schip[piece, :]
            after = own + d1 * carry[piece, :].astype(F32)
            msend[piece, :] = (s0buf[piece, :].astype(F32) + d0 * after).astype(BF16)
            csend[piece, :] = after.astype(BF16)

            @pl.when(z > 0)
            def _():
                chain_copy(q).start()

            core_copy(q).start()

    @pl.when(ahead)
    def _():
        within_all()

    drain()
    gw_out = pltpu.make_async_copy(gw, gw_hbm, l_sem.at[1])
    gw_out.start()

    @pl.when(c == 0)
    def _():
        for q in range(4):
            core_copy(q).wait_recv()

    lane512 = lax.broadcasted_iota(jnp.int32, (1, 512), 1) // 64
    skw = jnp.zeros((1, 512), F32)
    for h in range(8):
        skw = jnp.where(lane512 == h, skip_ref[0, h], skw)
    state = carry[...].astype(F32)
    for k in (3, 2, 1, 0):
        rows = slice(k * BLK, (k + 1) * BLK)
        across = jnp.dot(bsel[rows, :], state.astype(BF16), preferred_element_type=F32)
        if k:
            state = st[k] + ends[k] * state
        out = tsw[rows, :] * (ng[rows, :] + etw[rows, :] * across) + skw * gs[rows, :].astype(F32)
        so_rows = out.astype(BF16)
        if k == 3:
            gate_out.wait()
        so[rows, :] = so_rows
    x_out = pltpu.make_async_copy(so, gx_hbm, l_sem.at[2])
    x_out.start()

    for d in range(4):
        for k in range(9):
            a_copy(d, k, False).wait_send()
    for d in (0, 1):
        for k in range(7):
            w_copy(d, k, False).wait_send()
    for k in range(8):
        b_copy(k, False).wait_send()
    row_done(sqs, g_ssem, g_rsem)
    row_done(wds, d_ssem, d_rsem)
    r_done()

    @pl.when(c == 0)
    def _():
        d0_copy().wait_send()
        s0_copy().wait_send()

    @pl.when(c == 1)
    def _():
        for q in range(4):
            core_copy(q).wait_send()

            @pl.when(z > 0)
            def _():
                chain_copy(q).wait_send()

    gw_out.wait()
    x_out.wait()


def on_device(a, w, so, gt, nw, ts, ld, bin_, cin, skip):
    any_ = pl.BlockSpec(memory_space=pl.ANY)
    vmem = pl.BlockSpec(memory_space=pltpu.VMEM)
    smem = pl.BlockSpec(memory_space=pltpu.SMEM)
    V, D = pltpu.VMEM, pltpu.SemaphoreType.DMA
    gx, gg, gwt = pl.pallas_call(
        kernel,
        out_shape=(
            jax.ShapeDtypeStruct((1024, 512), BF16),
            jax.ShapeDtypeStruct((1024, 512), BF16),
            jax.ShapeDtypeStruct((512, 256), F32),
        ),
        in_specs=[any_, any_, any_, any_, vmem, vmem, vmem, any_, any_, smem],
        out_specs=(any_, any_, any_),
        scratch_shapes=[
            V((16, 1024, 256), BF16), V((16, 256, 512), BF16), V((1024, 512), BF16), V((1024, 512), BF16),
            V((1024, 512), F32), V((1024, 512), F32), V((1024, 512), F32), V((1024, 512), F32),
            V((1024, 512), F32), V((1024, 512), F32), V((1024, 512), F32), V((4, 8, 256, 256), BF16),
            V((8, 512, 256), BF16), V((8, 512, 256), BF16), V((8, 512, 256), BF16), V((8, 512, 256), BF16),
            V((8, 512, 256), BF16),
            V((512, 1024), BF16), V((2, 8192, 128), BF16), V((2048, 128), F32), V((1024, 128), BF16),
            V((1024, 128), BF16), V((128, 1024), BF16), V((1024, 128), F32), V((8, 1024), F32), V((1024, 128), F32),
            V((16, 1, 1024), F32), V((16, 1, 1024), F32), V((4, 128, 512), F32), V((128, 512), F32),
            V((128, 512), BF16), V((2, 1, 512), F32), V((128, 512), BF16), V((128, 512), BF16), V((128, 512), BF16),
            V((512, 256), F32),
            D((4, 9)), D((4, 9)), D((2, 7)), D((2, 7)), D((8,)), D((8,)), D((8, 2)), D((8, 2, 2)), D((16,)), D((16,)),
            D((8,)), D((8,)), D((16,)), D((16,)), D((2,)), D((2,)), D((4,)), D((4,)), D((4,)), D((6,)),
        ],
        compiler_params=pltpu.CompilerParams(
            collective_id=0, has_side_effects=True, vmem_limit_bytes=67043328
        ),
        name="mixer_backward",
    )(
        a, w, so, gt, nw.reshape(1, 512), ts, ld, bin_.reshape(8192, 128), cin.reshape(8192, 128), skip.reshape(1, 8)
    )
    return gx, gg, gwt.T


def solution(mesh):
    finer = Mesh(mesh.devices.reshape(8, 2, 4, 4), ("z", "c", "x", "y"))
    seq, heads = ("z", "c"), ("x", "y")
    return jax.shard_map(
        on_device,
        mesh=finer,
        in_specs=(
            P(seq, heads), P(seq, heads), P(seq, heads), P(seq, heads), P(heads), P(heads, seq), P(heads, seq),
            P(seq, None, None), P(seq, None, None), P(heads),
        ),
        out_specs=(P(seq, heads), P(seq, heads), P(seq, heads)),
        check_vma=False,
    )
```

time: 295 us -> 113 us (0.38); the launches traced: 291 us -> 113 us
  waiting for transfers between devices: 167 us -> 0 us
  Pallas kernels: 0 us -> 107 us
  matrix products: 39.5 us -> 0 us
  blocking collectives: 38 us -> 0 us
  other arithmetic: 15.8 us -> 0 us
  between operations: 15.3 us -> 0.65 us
  local copies, waits for them, and re-layouts: 14.4 us -> 5.36 us
    all_gather x3 -> x0, waiting for transfers between devices: 109 us -> none  [the longest x1 79.6 us: on_device(): full_grad = lax.all_gather(grad_output, HEAD, axis=1, tiled=True)]
    pallas_call x0 -> x1, Pallas kernels: none -> 107 us  [on_device(): pl.pallas_call(kernel, out_shape=(jax.ShapeDtypeStruct((1024, 512), BF16)...]
    reduce_scatter x1 -> x0, waiting for transfers between devices: 56.8 us -> none  [on_device(): lax.psum_scatter(lax.dot_general(columns, normed, (((0,), (0,)), ((), ())...]
    dot_general x7 -> x0, matrix products: 39.5 us -> none  [the longest x1 11.3 us: on_device(): jnp.dot(columns, lax.all_gather(out_weight, SEQ, axis=0, tiled=True), pre...]
    unnamed x2 -> x0, blocking collectives: 17.7 us -> none
    psum x2 -> x0, blocking collectives: 12.5 us -> none  [over_axes(): x = lax.psum(x, axis)]
    all_gather x1 -> x0, blocking collectives: 7.85 us -> none  [carried_in(): pieces = jax.tree.map(lambda part: lax.all_gather(part, axis), running)]
    unnamed x32 -> x5, local copies, waits for them, and re-layouts: 13.2 us -> 5.36 us
  transfers between devices with their start and end apart: 4 -> 0, of which waited for: 3 -> 0; matrix products, arithmetic and copies ran while one was open for 15% -> 0% of each run, Pallas kernels for 0% -> 0%
where the time goes in v1:
time: 113 us
  Pallas kernels  107 us (95%)
  local copies, waits for them, and re-layouts  5.36 us (5%)
    pallas_call x1, Pallas kernels, on_device(): pl.pallas_call(kernel, out_shape=(jax.ShapeDtypeStruct((1024, 512), BF16)...  107 us
    unnamed x5, local copies, waits for them, and re-layouts  5.36 us

profile of v1, /device:TPU:21, one launch (start us, length us, event | category | flops | bytes accessed | tf_op | source)
XLA Modules:
  0.0 113.0 jit_solution(7578875687265334370)
XLA Ops:
  0.6 107.0 %mixer_backward.1 = (bf16[1024,512]{1,0:T(8,128)(2,1)}, bf16[1024,512]{1,0:T(8,128)(2,1)}, f32[512,256]{1,0:T(8,128)}) custom-call(bf16[1024,256]{1,0:T(8,128)(2,1)} %a_hbm.1, bf16[256,512]{1,0:T(8,128)(2,1)} %w_hbm.1, bf16[1024,512]{1,0:T(8,128)(2,1)} %so_hbm.1, bf16[1024,512]{1,0:T(8,128)(2,1)} %gt_hbm.1, f32[1,512]{1,0:T(1,128)} %bitcast.8, ...), custom_call_target="tpu_custom_call" | custom-call | tf_op jit(solution)/shard_map/mixer_backward/pallas_call | solution.py:623
  107.6 0.0 copy-start
  107.6 2.1 %copy.13 = f32[256,512]{1,0:T(8,128)} copy(f32[256,512]{0,1:T(8,128)} %bitcast.7) | data formatting | bytes 1048576
  109.7 2.3 %copy.16 = bf16[1024,512]{1,0:T(8,128)(2,1)} copy(bf16[1024,512]{1,0:T(8,128)(2,1)} %get-tuple-element.15) | data formatting | bytes 2097152
  112.0 0.0 copy-done
  112.0 1.0 copy.17
Async XLA Ops:
  107.6 4.4 %copy-start = (bf16[1024,512]{1,0:T(8,128)(2,1)S(1)}, bf16[1024,512]{1,0:T(8,128)(2,1)}, u32[]{:S(2)}) copy-start(bf16[1024,512]{1,0:T(8,128)(2,1)} %get-tuple-element.16) | copy-start | bytes 3145732

commit v2 on v1

v2 whole, which is shorter than its diff:
```python
import functools
import math

import jax
import jax.numpy as jnp
from jax import lax
from jax.experimental import pallas as pl
from jax.experimental.pallas import tpu as pltpu
from jax.sharding import Mesh
from jax.sharding import PartitionSpec as P

EPS = 1e-05
F32, BF16 = jnp.float32, jnp.bfloat16
MESH = pl.DeviceIdType.MESH
BLK = 256
A, B = (0, 512), (512, 512)
A0, A1, B0, B1 = (0, 256), (256, 256), (512, 256), (768, 256)
STEP = ((1, 0), (-1, 0), (0, 1), (0, -1))
ITEMS = (
    ((0, 0, A), (0, 0, B), (-1, 0, A), (0, 1, B), (0, -1, B), (0, 2, B), (-1, 1, B0), (-1, -1, B0), (-1, 2, B0)),
    ((0, 0, A), (0, 0, B), (1, 0, B), (0, 1, B), (0, -1, B), (0, 2, B), (1, 1, B1), (1, -1, B1), (1, 2, B1)),
    ((0, 0, B), (0, 0, A), (0, -1, A), (1, 0, A), (-1, 0, A), (2, 0, A), (1, -1, A0), (-1, -1, A0), (2, -1, A0)),
    ((0, 0, B), (0, 0, A), (0, 1, B), (1, 0, A), (-1, 0, A), (2, 0, A), (1, 1, A1), (-1, 1, A1), (2, 1, A1)),
)
PAIRS = (
    ((0, 0), (0, 1)),
    ((1, 0), (0, -1)),
    ((-1, 0), (1, 1)),
    ((2, 0), (-1, 1)),
    ((0, 2), (1, -1)),
    ((1, 2), (-1, -1)),
    ((-1, 2), (2, 1)),
    ((2, 2), (2, -1)),
)
ECUM, ETAIL, TSTEP, CUM = 0, 24, 48, 72


def split3(q):
    first = q.astype(BF16).astype(F32)
    second = (q - first).astype(BF16).astype(F32)
    third = (q - first - second).astype(BF16).astype(F32)
    return [first, second, third]


def scoped(fn):
    @functools.wraps(fn)
    def wrapped(*args):
        with jax.named_scope(fn.__name__):
            return fn(*args)

    return wrapped


def fold_lanes(v):
    return (v[:, 0:128] + v[:, 128:256]) + (v[:, 256:384] + v[:, 384:512])


def kernel(
    a_hbm, w_hbm, so_hbm, gt_hbm, nw_ref, ts_ref, ld_ref, bin_hbm, cin_hbm, skip_ref,
    gx_hbm, gg_hbm, gw_hbm,
    abuf, wbuf, so, gt, gated, silu, fgate, ng, ecw, etw, tsw, wts, gkeep, gout, gin, fromz,
    normt, stage, conv, bsel, csel, ct, qt, cum_s, col, sqs, wds, st, acc, s0buf, d0buf, sall, dall, weight, carry, gw,
    a_ssem, a_rsem, w_ssem, w_rsem, b_ssem, b_rsem, r_ssem, r_rsem, g_ssem, g_rsem, h_ssem, h_rsem,
    d_ssem, d_rsem, s_ssem, s_rsem, c_ssem, c_rsem, m_ssem, m_rsem, e_ssem, e_rsem, l_sem,
):
    z, c, x, y = (lax.axis_index(n) for n in ("z", "c", "x", "y"))
    head = x * 4 + y

    def at(dz=0, dc=0, dx=0, dy=0):
        return ((z + dz + 8) % 8, (c + dc) % 2, (x + dx + 4) % 4, (y + dy + 4) % 4)

    def slot(dx, dy):
        return ((x + dx + 4) % 4) * 4 + (y + dy + 4) % 4

    def remote(src, dst, ssem, rsem, dev):
        return pltpu.make_async_remote_copy(
            src_ref=src, dst_ref=dst, send_sem=ssem, recv_sem=rsem, device_id=dev, device_id_type=MESH
        )

    loads = [
        pltpu.make_async_copy(a_hbm, abuf.at[head], l_sem.at[0]),
        pltpu.make_async_copy(w_hbm, wbuf.at[z * 2 + c], l_sem.at[1]),
        pltpu.make_async_copy(so_hbm, so, l_sem.at[2]),
        pltpu.make_async_copy(gt_hbm, gt, l_sem.at[3]),
        pltpu.make_async_copy(bin_hbm, stage.at[0], l_sem.at[4]),
        pltpu.make_async_copy(cin_hbm, stage.at[1], l_sem.at[5]),
    ]
    for load in loads:
        load.start()
    barrier = pltpu.get_barrier_semaphore()

    def greet(k, carry_):
        other = (head + k) % 16
        pl.semaphore_signal(barrier, inc=1, device_id=(z, c, other // 4, other % 4), device_id_type=MESH)
        return carry_

    lax.fori_loop(1, 16, greet, 0)
    for dev in (at(dz=1), at(dz=-1), at(dc=1)):
        pl.semaphore_signal(barrier, inc=1, device_id=dev, device_id_type=MESH)
    with jax.named_scope("entry"):
        loads[0].wait()
        loads[1].wait()
        pl.semaphore_wait(barrier, 18)

    def a_copy(d, k, got):
        dx, dy, (row, n) = ITEMS[d][k]
        sx, sy = STEP[d]
        here = slot(dx - sx, dy - sy) if got else slot(dx, dy)
        piece = abuf.at[here, pl.ds(row, n)]
        return remote(piece, piece, a_ssem.at[d, k], a_rsem.at[d, k], at(dx=sx, dy=sy))

    def a_send(*flows):
        for d, k in flows:
            a_copy(d, k, False).start()

    @scoped
    def a_wait(*flows):
        for d, k in flows:
            a_copy(d, k, True).wait_recv()

    every = lambda k: [(d, k) for d in range(4)]

    def w_copy(d, k, got):
        sign = 1 if d == 0 else -1
        far = (k // 2 if k < 6 else 3) + (1 if got else 0)
        half = k % 2 if k < 6 else d
        here = ((z - sign * far + 8) % 8) * 2 + c
        piece = wbuf.at[here, pl.ds(half * 128, 128)]
        return remote(piece, piece, w_ssem.at[d, k], w_rsem.at[d, k], at(dz=sign))

    def b_copy(k, got):
        here = ((z + k) % 8) * 2 + ((c + 1) % 2 if got else c)
        return remote(wbuf.at[here], wbuf.at[here], b_ssem.at[k], b_rsem.at[k], at(dc=1))

    @scoped
    def w_event(k):
        for d in (0, 1):
            w_copy(d, k, True).wait_recv()
            if k < 4:
                w_copy(d, k + 2, False).start()
        if k == 4:
            w_copy(0, 6, False).start()
        if k == 5:
            w_copy(1, 6, False).start()
        if k in (1, 3, 5):
            b_copy((k + 1) // 2, False).start()
            b_copy(8 - (k + 1) // 2, False).start()
        if k == 6:
            b_copy(4, False).start()

    def row_copy(slots, ssem, rsem, k, got):
        other = (head + k) % 16
        source = (head + 16 - k) % 16
        here = source if got else head
        return remote(slots.at[here], slots.at[here], ssem.at[k], rsem.at[k], (z, c, other // 4, other % 4))

    def row_send(slots, ssem, rsem):
        def one(k, carry_):
            row_copy(slots, ssem, rsem, k, False).start()
            return carry_

        lax.fori_loop(1, 16, one, 0)

    @scoped
    def row_sum(slots, ssem, rsem):
        def one(k, carry_):
            copy = row_copy(slots, ssem, rsem, k, True)
            copy.wait_recv()
            return carry_

        lax.fori_loop(1, 16, one, 0)
        total = slots[0]
        for k in range(1, 16):
            total = total + slots[k]
        return total

    def row_done(slots, ssem, rsem):
        def one(k, carry_):
            row_copy(slots, ssem, rsem, k, False).wait_send()
            return carry_

        lax.fori_loop(1, 16, one, 0)

    def to_column(row):
        return jnp.broadcast_to(row, (128, row.shape[1])).T

    def rows128(r):
        return pl.ds(pl.multiple_of(r * 128, 128), 128)

    @scoped
    def gate_phase():
        loads[2].wait()
        loads[3].wait()

        @pl.loop(0, 8)
        def _(r):
            rows = rows128(r)
            values = so[rows, :].astype(F32)
            gate_values = gt[rows, :].astype(F32)
            sig = jax.nn.sigmoid(gate_values)
            sl = gate_values * sig
            gv = values * sl
            gated[rows, :] = gv
            silu[rows, :] = sl
            fgate[rows, :] = values * sig * (1.0 + gate_values * (1.0 - sig))
            sqs[head, :, rows] = jnp.sum(fold_lanes(gv * gv).T, axis=0, keepdims=True)

    rows_i = lax.broadcasted_iota(jnp.int32, (BLK, BLK), 0)
    cols_i = lax.broadcasted_iota(jnp.int32, (BLK, BLK), 1)

    @scoped
    def per_head():
        tri = (rows_i <= cols_i).astype(F32).astype(BF16)
        for k in range(4):
            cols = slice(k * BLK, (k + 1) * BLK)
            parts = jnp.concatenate(split3(ld_ref[:, cols]), axis=0).astype(BF16)
            summed = jnp.dot(parts, tri, preferred_element_type=F32)
            cum = summed[0:8] + summed[8:16] + summed[16:24]
            cum_s[:, cols] = cum
            total = cum[:, BLK - 1 : BLK]
            table = (
                split3(jnp.exp(cum))
                + split3(jnp.exp(total - cum))
                + split3(ts_ref[:, cols])
                + [cum, jnp.zeros((128 - CUM - 8, BLK), F32)]
            )
            qt[cols, :] = jnp.concatenate(table, axis=0).T
        lane_head = lax.broadcasted_iota(jnp.int32, (128, 512), 1) // 64
        part_row = lax.broadcasted_iota(jnp.int32, (128, 512), 0)

        for first, wide in ((ECUM, ecw), (ETAIL, etw), (TSTEP, tsw)):
            inside = (part_row >= first) & (part_row < first + 24) & ((part_row - first) % 8 == lane_head)
            chosen = inside.astype(F32).astype(BF16)

            @pl.loop(0, 4)
            def _(k, chosen=chosen, wide=wide):
                rows = pl.ds(pl.multiple_of(k * BLK, BLK), BLK)
                wide[rows, :] = jnp.dot(qt[rows, :].astype(BF16), chosen, preferred_element_type=F32)

        d0buf[0] = ecw[255:256, :] * ecw[511:512, :] * ecw[767:768, :] * ecw[1023:1024, :]

    @scoped
    def pick_group():
        group = head // 2
        for which, (load, sel) in enumerate(((loads[4], bsel), (loads[5], csel))):
            load.wait()

            @pl.loop(0, 4)
            def _(r, which=which, sel=sel):
                conv[...] = stage[which, pl.ds(pl.multiple_of(r * 2048, 2048), 2048), :].astype(F32)
                sel[pl.ds(pl.multiple_of(r * 256, 256), 256), :] = conv[pl.ds(group, 256, stride=8), :].astype(BF16)

        ct[...] = csel[...].astype(F32).T.astype(BF16)

    @scoped
    def block_weights():
        keep_upper = cols_i >= rows_i

        @pl.loop(0, 4)
        def _(k):
            rows = pl.ds(pl.multiple_of(k * BLK, BLK), BLK)
            scores = lax.dot_general(
                bsel[rows, :], csel[rows, :], (((1,), (1,)), ((), ())), preferred_element_type=F32
            )
            columns = qt[rows, :]
            for h in range(8):
                gap = cum_s[h : h + 1, rows] - columns[:, CUM + h : CUM + h + 1]
                decayed = jnp.where(keep_upper, scores * jnp.exp(jnp.minimum(gap, 0.0)), 0.0)
                wts[k, h] = decayed.astype(BF16)

    @scoped
    def normalize(mean):
        col[...] = to_column(lax.rsqrt(mean + EPS))
        nw = nw_ref[...]

        @pl.loop(0, 8)
        def _(r):
            rows = rows128(r)
            normed = gated[rows, :] * col[rows, :][:, 0:1] * nw
            normt[:, rows] = normed.T.astype(BF16)

    def pair_slots(p):
        (ex, ey), (ox, oy) = PAIRS[p]
        return slot(ex, ey), slot(ox, oy)

    def mine_and_other(p):
        first, second = pair_slots(p)
        same = (y + PAIRS[p][0][1] + 4 + c) % 2 == 0
        return jnp.where(same, first, second), jnp.where(same, second, first)

    def give_copy(p):
        return remote(gout.at[p], gin.at[p], h_ssem.at[p], h_rsem.at[p], at(dc=1))

    @scoped
    def weight_part(p):
        mine, other = mine_and_other(p)

        @pl.loop(0, 4)
        def _(r):
            rows = rows128(r)
            lhs = normt[rows, :]
            gout[p, rows, :] = jnp.dot(lhs, abuf[other], preferred_element_type=F32).astype(BF16)
            gkeep[p, rows, :] = jnp.dot(lhs, abuf[mine], preferred_element_type=F32).astype(BF16)

        give_copy(p).start()

    @scoped
    def grad_part(p):
        first, second = pair_slots(p)

        @pl.loop(0, 4)
        def _(r):
            rows = pl.ds(pl.multiple_of(r * 256, 256), 256)
            add = jnp.dot(abuf[first, rows, :], wbuf[first], preferred_element_type=F32)
            add = add + jnp.dot(abuf[second, rows, :], wbuf[second], preferred_element_type=F32)
            if p == 0:
                ng[rows, :] = add
            else:
                ng[rows, :] += add

    def among(i, values):
        found = values[0]
        for q in range(1, len(values)):
            found = jnp.where(i == q, values[q], found)
        return found

    roots = [mine_and_other(p)[0] // 2 for p in range(8)]

    def r_copy(p, i, way):
        piece = pl.ds(i * 256, 256)
        dev = ((z + jnp.where(way == 0, 1, 7)) % 8, c, x, y)
        return remote(gkeep.at[p, piece], fromz.at[way, p, piece], r_ssem.at[p, i], r_rsem.at[p, i, way], dev)

    @scoped
    def combine(p):
        give_copy(p).wait_recv()
        gkeep[p] = (gkeep[p].astype(F32) + gin[p].astype(F32)).astype(BF16)

    def rs_level(p, lev):
        rel = (z - among(p, roots) + 8) % 8
        for i in (0, 1):
            piece = pl.ds(i * 256, 256)
            way = jnp.where(rel >= 4 + i, 0, 1)
            level = jnp.where(rel >= 4 + i, rel - (4 + i), (3 + i) - rel)

            @pl.when((rel != 0) & (level == lev))
            def _():
                copy = r_copy(p, i, way)

                @pl.when(lev > 0)
                def _():
                    copy.wait_recv()
                    gkeep[p, piece, :] = (
                        gkeep[p, piece, :].astype(F32) + fromz[way, p, piece, :].astype(F32)
                    ).astype(BF16)

                copy.start()

        @pl.when((rel == 0) & (lev == 4))
        def _():
            for i in (0, 1):
                piece = pl.ds(i * 256, 256)
                r_copy(p, i, 0).wait_recv()
                r_copy(p, i, 1).wait_recv()
                total = (
                    gkeep[p, piece, :].astype(F32)
                    + fromz[0, p, piece, :].astype(F32)
                    + fromz[1, p, piece, :].astype(F32)
                )
                gw[:, i * 256 : i * 256 + 256] = total.T * (1.0 / math.sqrt(16384.0))

    @scoped
    def rs_stage(*steps):
        for p, lev in steps:
            if lev == 0:
                combine(p)
        ps, levs = [p for p, _ in steps], [lev for _, lev in steps]

        def one(i, carry_):
            rs_level(among(i, ps), among(i, levs))
            return carry_

        lax.fori_loop(0, len(steps), one, 0)

    def hop_copy(buf, ssem, rsem, way, d, got, *rest):
        source = z + (d if got else d - 1) if way == 1 else (z + 8 - (d if got else d - 1)) % 8
        here = jnp.minimum(source, 7)
        piece = buf.at[(here, *rest)]
        index = (way, d - 1)
        if rest:
            index = (way, d - 1, rest[0].start // 64)
        return remote(piece, piece, ssem.at[index], rsem.at[index], ((z + (1 if way == 0 else 7)) % 8, 1, x, y))

    def hop_valid(way, d, got):
        if way == 1:
            return (z + d <= 7) if got else ((z > 0) & (z + d - 1 <= 7))
        return (z + 8 - (d if got else d - 1)) % 8 >= 5

    WAYS = ((1, 1), (0, 1), (1, 2), (0, 2), (1, 3), (0, 3), (1, 4))
    HALVES = (pl.ds(0, 64), pl.ds(64, 64))

    def decay_copy(way, d, got):
        return hop_copy(dall, e_ssem, e_rsem, way, d, got)

    def state_copy(way, d, got, half):
        return hop_copy(sall, m_ssem, m_rsem, way, d, got, half)

    def decay_hop(d):
        @pl.when(c == 1)
        def _():
            for way in (1, 0):
                if d and (way, d) in WAYS:

                    @pl.when(hop_valid(way, d, True))
                    def _():
                        decay_copy(way, d, True).wait_recv()

                if (way, d + 1) in WAYS:

                    @pl.when(hop_valid(way, d + 1, False))
                    def _():
                        decay_copy(way, d + 1, False).start()

    @scoped
    def state_hop(d):
        for half in HALVES:
            for way in (1, 0):
                if d and (way, d) in WAYS:

                    @pl.when(hop_valid(way, d, True))
                    def _():
                        state_copy(way, d, True, half).wait_recv()

                if (way, d + 1) in WAYS:

                    @pl.when(hop_valid(way, d + 1, False))
                    def _():
                        state_copy(way, d + 1, False, half).start()

    def hops_done():
        for way, d in WAYS:

            @pl.when(hop_valid(way, d, False))
            def _():
                decay_copy(way, d, False).wait_send()
                for half in HALVES:
                    state_copy(way, d, False, half).wait_send()

    def s0_copy():
        return remote(s0buf.at[0], s0buf.at[1], s_ssem.at[0], s_rsem.at[0], (z, 1, x, y))

    def d0_copy():
        return remote(d0buf.at[0], d0buf.at[1], s_ssem.at[1], s_rsem.at[1], (z, 1, x, y))

    def core_copy():
        return remote(carry.at[0], carry.at[1], c_ssem.at[0], c_rsem.at[0], (z, 0, x, y))

    a_send(*every(0))
    for k in (0, 1):
        for d in (0, 1):
            w_copy(d, k, False).start()
    b_copy(0, False).start()
    gate_phase()
    row_send(sqs, g_ssem, g_rsem)
    a_send(*every(1))
    per_head()

    @pl.when(c == 0)
    def _():
        d0_copy().start()

    w_event(0)
    pick_group()
    w_event(1)
    a_wait(*every(0))
    a_send((0, 2), (0, 3), (0, 4), (1, 3), (3, 2), (3, 3), (3, 4), (2, 3))
    block_weights()
    w_event(2)

    @pl.when(c == 1)
    def _():
        d0_copy().wait_recv()
        dall[z] = d0buf[0] * d0buf[1]

    normalize(row_sum(sqs, g_ssem, g_rsem) * (1.0 / 8192))
    w_event(3)
    decay_hop(0)
    a_wait(*every(1))
    a_send((1, 2), (1, 4), (2, 2), (2, 4))
    weight_part(0)
    w_event(4)
    weight_part(1)
    w_event(5)
    decay_hop(1)
    a_wait((0, 2), (3, 2), (1, 3), (2, 3))
    a_send(*every(5))
    rs_stage((0, 0), (1, 0))
    w_event(6)
    decay_hop(2)
    a_wait((0, 3), (1, 2), (2, 2), (3, 3))
    a_send(*every(6))
    weight_part(2)
    with jax.named_scope("b_wait"):
        for k in range(8):
            b_copy(k, True).wait_recv()
    decay_hop(3)
    grad_part(0)
    grad_part(1)
    grad_part(2)
    decay_hop(4)
    a_wait(*every(4))
    a_send(*every(7))
    rs_stage((0, 1), (1, 1), (2, 0))
    weight_part(3)
    grad_part(3)
    weight_part(4)
    grad_part(4)
    a_wait(*every(5))
    a_send(*every(8))
    rs_stage((0, 2), (1, 2), (2, 1), (3, 0), (4, 0))
    a_wait(*every(6))
    weight_part(5)
    grad_part(5)
    a_wait(*every(7))
    grad_part(6)
    weight_part(6)
    rs_stage((0, 3), (1, 3), (2, 2), (3, 1), (4, 1), (5, 0))
    a_wait(*every(8))
    grad_part(7)

    with jax.named_scope("weighted"):

        @pl.loop(0, 8)
        def _(r):
            rows = rows128(r)
            term = nw_ref[...] * ng[rows, :] * gated[rows, :]
            wds[head, :, rows] = jnp.sum(fold_lanes(term).T, axis=0, keepdims=True)

    row_send(wds, d_ssem, d_rsem)
    weight_part(7)
    rs_stage((6, 0))

    @pl.when(c == 1)
    def _():
        weight[1] = jnp.ones((1, 512), F32)
        for k in range(2, 8):

            @pl.when(z + k <= 7)
            def _():
                weight[k] = weight[k - 1] * dall[jnp.minimum(z + k - 1, 7)]

    weighted = row_sum(wds, d_ssem, d_rsem)

    gs = gt
    with jax.named_scope("grads"):
        cube = to_column(weighted * (1.0 / 8192))
        for r in range(8):
            rows = slice(r * 128, (r + 1) * 128)
            inv = col[rows, 0:1]
            wcol = cube[rows, 0:1]
            gg = inv * nw_ref[...] * ng[rows, :] - gated[rows, :] * (inv * inv * inv * wcol)
            so[rows, :] = (gg * fgate[rows, :]).astype(BF16)
            gs[rows, :] = (gg * silu[rows, :]).astype(BF16)
    gate_out = pltpu.make_async_copy(so, gg_hbm, l_sem.at[0])
    gate_out.start()

    ends = [ecw[k * BLK + BLK - 1 : k * BLK + BLK, :] for k in range(4)]

    def summary():
        return st[0] + ends[0] * (st[1] + ends[1] * (st[2] + ends[2] * st[3]))

    with jax.named_scope("states"):

        @pl.loop(0, 4)
        def _(k):
            rows = pl.ds(pl.multiple_of(k * BLK, BLK), BLK)
            scaled = (ecw[rows, :] * gs[rows, :].astype(F32)).astype(BF16)
            st[k] = jnp.dot(ct[:, rows], scaled, preferred_element_type=F32)

    @pl.when(c == 0)
    def _():
        s0buf[0] = summary().astype(BF16)
        s0_copy().start()

    rs_stage((7, 0))

    @pl.when(c == 1)
    def _():
        own = d0buf[1] * summary()
        with jax.named_scope("s0_wait"):
            s0_copy().wait_recv()
        sall[z] = (s0buf[1].astype(F32) + own).astype(BF16)
        state_hop(0)

    @scoped
    def within_all():
        low = lax.broadcasted_iota(jnp.int32, (BLK, 128), 1) < 64

        @pl.loop(0, 4)
        def _(k):
            rows = pl.ds(pl.multiple_of(k * BLK, BLK), BLK)
            for hp in range(4):
                cols = slice(hp * 128, hp * 128 + 128)
                g = gs[rows, cols]
                zero = jnp.zeros_like(g)
                ng[rows, cols] = jnp.dot(
                    wts[k, 2 * hp], jnp.where(low, g, zero), preferred_element_type=F32
                ) + jnp.dot(wts[k, 2 * hp + 1], jnp.where(low, zero, g), preferred_element_type=F32)

    within_all()

    def take(k):
        @pl.when(z + k <= 7)
        def _():
            acc[...] += weight[k] * sall[jnp.minimum(z + k, 7)].astype(F32)

    def hop_and_take(d):
        @pl.when(c == 1)
        def _():
            state_hop(d)
            if d == 1:
                acc[...] = jnp.zeros((128, 512), F32)
            take(d)
            if d < 4:
                take(8 - d)

    hop_and_take(1)
    rs_stage((0, 4), (1, 4), (2, 3), (3, 2), (4, 2), (5, 1), (6, 1), (7, 1))
    hop_and_take(2)
    with jax.named_scope("sends_1"):
        for d in range(4):
            for k in range(9):
                a_copy(d, k, False).wait_send()
        for d in (0, 1):
            for k in range(7):
                w_copy(d, k, False).wait_send()
        for k in range(8):
            b_copy(k, False).wait_send()
        row_done(sqs, g_ssem, g_rsem)
    hop_and_take(3)
    rs_stage((2, 4), (3, 3), (4, 3), (5, 2), (6, 2), (7, 2))
    hop_and_take(4)

    @pl.when(c == 1)
    def _():
        own = st[0] + ends[0] * (st[1] + ends[1] * (st[2] + ends[2] * st[3]))
        carry[0] = (own + d0buf[0] * acc[...]).astype(BF16)
        core_copy().start()

    rs_stage((3, 4), (4, 4), (5, 3), (6, 3), (7, 3))

    @pl.when(c == 0)
    def _():
        with jax.named_scope("core_wait"):
            core_copy().wait_recv()
        acc[...] = carry[1].astype(F32)

    with jax.named_scope("final"):
        lane512 = lax.broadcasted_iota(jnp.int32, (1, 512), 1) // 64
        skw = jnp.zeros((1, 512), F32)
        for h in range(8):
            skw = jnp.where(lane512 == h, skip_ref[0, h], skw)
        gate_out.wait()
        state = acc[...]
        for k in (3, 2, 1, 0):
            rows = slice(k * BLK, (k + 1) * BLK)
            across = jnp.dot(bsel[rows, :], state.astype(BF16), preferred_element_type=F32)
            if k:
                state = st[k] + ends[k] * state
            out = tsw[rows, :] * (ng[rows, :] + etw[rows, :] * across) + skw * gs[rows, :].astype(F32)
            so[rows, :] = out.astype(BF16)
        x_out = pltpu.make_async_copy(so, gx_hbm, l_sem.at[2])
        x_out.start()

    rs_stage((5, 4), (6, 4), (7, 4))
    gw_out = pltpu.make_async_copy(gw, gw_hbm, l_sem.at[1])
    gw_out.start()

    with jax.named_scope("sends_2"):
        row_done(wds, d_ssem, d_rsem)

        def one(p, carry_):
            @pl.when((z - among(p, roots) + 8) % 8 != 0)
            def _():
                for i in (0, 1):
                    r_copy(p, i, 0).wait_send()

            give_copy(p).wait_send()
            return carry_

        lax.fori_loop(0, 8, one, 0)

        @pl.when(c == 0)
        def _():
            d0_copy().wait_send()
            s0_copy().wait_send()

        @pl.when(c == 1)
        def _():
            core_copy().wait_send()
            hops_done()

        gw_out.wait()
        x_out.wait()


def on_device(a, w, so, gt, nw, ts, ld, bin_, cin, skip):
    any_ = pl.BlockSpec(memory_space=pl.ANY)
    vmem = pl.BlockSpec(memory_space=pltpu.VMEM)
    smem = pl.BlockSpec(memory_space=pltpu.SMEM)
    V, D = pltpu.VMEM, pltpu.SemaphoreType.DMA
    return pl.pallas_call(
        kernel,
        out_shape=(
            jax.ShapeDtypeStruct((1024, 512), BF16),
            jax.ShapeDtypeStruct((1024, 512), BF16),
            jax.ShapeDtypeStruct((256, 512), F32),
        ),
        in_specs=[any_, any_, any_, any_, vmem, vmem, vmem, any_, any_, smem],
        out_specs=(any_, any_, any_),
        scratch_shapes=[
            V((16, 1024, 256), BF16), V((16, 256, 512), BF16), V((1024, 512), BF16), V((1024, 512), BF16),
            V((1024, 512), F32), V((1024, 512), F32), V((1024, 512), F32), V((1024, 512), F32),
            V((1024, 512), F32), V((1024, 512), F32), V((1024, 512), F32), V((4, 8, 256, 256), BF16),
            V((8, 512, 256), BF16), V((8, 512, 256), BF16), V((8, 512, 256), BF16), V((2, 8, 512, 256), BF16),
            V((512, 1024), BF16), V((2, 8192, 128), BF16), V((2048, 128), F32), V((1024, 128), BF16),
            V((1024, 128), BF16), V((128, 1024), BF16), V((1024, 128), F32), V((8, 1024), F32), V((1024, 128), F32),
            V((16, 1, 1024), F32), V((16, 1, 1024), F32), V((4, 128, 512), F32), V((128, 512), F32),
            V((2, 128, 512), BF16), V((2, 1, 512), F32), V((8, 128, 512), BF16), V((8, 1, 512), F32),
            V((8, 1, 512), F32), V((2, 128, 512), BF16), V((256, 512), F32),
            D((4, 9)), D((4, 9)), D((2, 7)), D((2, 7)), D((8,)), D((8,)), D((8, 2)), D((8, 2, 2)), D((16,)), D((16,)),
            D((8,)), D((8,)), D((16,)), D((16,)), D((2,)), D((2,)), D((1,)), D((1,)), D((2, 4, 2)), D((2, 4, 2)),
            D((2, 4)), D((2, 4)), D((6,)),
        ],
        compiler_params=pltpu.CompilerParams(
            collective_id=0, has_side_effects=True, vmem_limit_bytes=67043328
        ),
        name="mixer_backward",
    )(
        a, w, so, gt, nw.reshape(1, 512), ts, ld, bin_.reshape(8192, 128), cin.reshape(8192, 128), skip.reshape(1, 8)
    )


def solution(mesh):
    finer = Mesh(mesh.devices.reshape(8, 2, 4, 4), ("z", "c", "x", "y"))
    seq, heads = ("z", "c"), ("x", "y")
    return jax.shard_map(
        on_device,
        mesh=finer,
        in_specs=(
            P(seq, heads), P(seq, heads), P(seq, heads), P(seq, heads), P(heads), P(heads, seq), P(heads, seq),
            P(seq, None, None), P(seq, None, None), P(heads),
        ),
        out_specs=(P(seq, heads), P(seq, heads), P(seq, heads)),
        check_vma=False,
    )
```

time: 113 us -> 99 us (0.88)
  the two profiles are of different devices: /device:TPU:21 before, /device:TPU:45 now
where the time goes in v2:
time: 99 us; the launch traced here: 98.8 us
  Pallas kernels  94 us (95%)
  local copies, waits for them, and re-layouts  4.15 us (4%)
    pallas_call x1, Pallas kernels, on_device(): pl.pallas_call(kernel, out_shape=(jax.ShapeDtypeStruct((1024, 512), BF16)...  94 us
    unnamed x7, local copies, waits for them, and re-layouts  4.15 us

profile of v2, /device:TPU:45, one launch (start us, length us, event | category | flops | bytes accessed | tf_op | source)
XLA Modules:
  0.0 98.8 jit_solution(13825431075266840256)
XLA Ops:
  0.6 94.0 %mixer_backward.1 = (bf16[1024,512]{1,0:T(8,128)(2,1)}, bf16[1024,512]{1,0:T(8,128)(2,1)}, f32[256,512]{1,0:T(8,128)}) custom-call(bf16[1024,256]{1,0:T(8,128)(2,1)} %a_hbm.1, bf16[256,512]{1,0:T(8,128)(2,1)} %w_hbm.1, bf16[1024,512]{1,0:T(8,128)(2,1)} %so_hbm.1, bf16[1024,512]{1,0:T(8,128)(2,1)} %gt_hbm.1, f32[1,512]{1,0:T(1,128)} %bitcast.6, ...), custom_call_target="tpu_custom_call" | custom-call | tf_op jit(solution)/shard_map/mixer_backward/pallas_call | solution.py:712
  94.6 0.0 copy-start
  94.6 0.0 copy-start.1
  94.7 2.4 %copy.16 = bf16[1024,512]{1,0:T(8,128)(2,1)} copy(bf16[1024,512]{1,0:T(8,128)(2,1)} %get-tuple-element.6) | data formatting | bytes 2097152
  97.0 0.0 copy-done
  97.0 1.0 copy.17
  98.0 0.0 copy-done.1
  98.0 0.8 copy.18
Async XLA Ops:
  94.6 2.4 %copy-start = (bf16[1024,512]{1,0:T(8,128)(2,1)S(1)}, bf16[1024,512]{1,0:T(8,128)(2,1)}, u32[]{:S(2)}) copy-start(bf16[1024,512]{1,0:T(8,128)(2,1)} %get-tuple-element.7) | copy-start | bytes 3145732
  94.6 3.4 %copy-start.1 = (f32[256,512]{1,0:T(8,128)S(1)}, f32[256,512]{1,0:T(8,128)}, u32[]{:S(2)}) copy-start(f32[256,512]{1,0:T(8,128)} %get-tuple-element.8) | copy-start | bytes 1572868

commit v3 on v2

--- a/solution.py
+++ b/solution.py
@@ -17,21 +17,23 @@
 A0, A1, B0, B1 = (0, 256), (256, 256), (512, 256), (768, 256)
 STEP = ((1, 0), (-1, 0), (0, 1), (0, -1))
 ITEMS = (
-    ((0, 0, A), (0, 0, B), (-1, 0, A), (0, 1, B), (0, -1, B), (0, 2, B), (-1, 1, B0), (-1, -1, B0), (-1, 2, B0)),
-    ((0, 0, A), (0, 0, B), (1, 0, B), (0, 1, B), (0, -1, B), (0, 2, B), (1, 1, B1), (1, -1, B1), (1, 2, B1)),
+    ((0, 0, A), (0, 0, B), (-1, 0, A), (0, 1, B), (0, -1, B), (0, 2, B0), (-1, 1, B0), (-1, -1, B0), (-1, 2, B0), (0, 2, B1)),
+    ((0, 0, A), (0, 0, B), (1, 0, B), (0, 1, B), (0, -1, B), (0, 2, B1), (1, 1, B1), (1, -1, B1), (1, 2, B1), (0, 2, B0)),
     ((0, 0, B), (0, 0, A), (0, -1, A), (1, 0, A), (-1, 0, A), (2, 0, A), (1, -1, A0), (-1, -1, A0), (2, -1, A0)),
     ((0, 0, B), (0, 0, A), (0, 1, B), (1, 0, A), (-1, 0, A), (2, 0, A), (1, 1, A1), (-1, 1, A1), (2, 1, A1)),
 )
-PAIRS = (
-    ((0, 0), (0, 1)),
-    ((1, 0), (0, -1)),
-    ((-1, 0), (1, 1)),
-    ((2, 0), (-1, 1)),
-    ((0, 2), (1, -1)),
-    ((1, 2), (-1, -1)),
-    ((-1, 2), (2, 1)),
-    ((2, 2), (2, -1)),
+BLOCKS = (
+    (0, 0), (0, 1), (1, 0), (0, -1), (-1, 0),
+    (2, 0), (0, 2), (1, 1),
+    (-1, 1), (1, -1), (-1, -1),
+    (2, 1), (2, -1),
+    (1, 2), (-1, 2),
+    (2, 2),
 )
+SPLIT = 8
+G0, G1, G2, G3, G4 = range(0, 5), range(5, 8), range(8, 11), range(11, 13), range(13, 16)
+G0A, G0B = (0, 2, 4), (1, 3)
+CUTS = [1] * 13 + [4] * 3
 ECUM, ETAIL, TSTEP, CUM = 0, 24, 48, 72
 
 
@@ -58,19 +60,19 @@
 def kernel(
     a_hbm, w_hbm, so_hbm, gt_hbm, nw_ref, ts_ref, ld_ref, bin_hbm, cin_hbm, skip_ref,
     gx_hbm, gg_hbm, gw_hbm,
-    abuf, wbuf, so, gt, gated, silu, fgate, ng, ecw, etw, tsw, wts, gkeep, gout, gin, fromz,
-    normt, stage, conv, bsel, csel, ct, qt, cum_s, col, sqs, wds, st, acc, s0buf, d0buf, sall, dall, weight, carry, gw,
+    abuf, wbuf, so, gt, gated, silu, fgate, ng, ecw, etw, tsw, wts, gkeep, gin, fromz, rootb,
+    normt, conv, bsel, csel, ct, qt, cum_s, col, sqs, wds, st, acc, s0buf, d0buf, sall, dall, weight, carry, gw,
     a_ssem, a_rsem, w_ssem, w_rsem, b_ssem, b_rsem, r_ssem, r_rsem, g_ssem, g_rsem, h_ssem, h_rsem,
-    d_ssem, d_rsem, s_ssem, s_rsem, c_ssem, c_rsem, m_ssem, m_rsem, e_ssem, e_rsem, l_sem,
+    d_ssem, d_rsem, s_ssem, s_rsem, c_ssem, c_rsem, m_ssem, m_rsem, e_ssem, e_rsem, o_ssem, o_rsem, l_sem,
 ):
     z, c, x, y = (lax.axis_index(n) for n in ("z", "c", "x", "y"))
     head = x * 4 + y
 
     def at(dz=0, dc=0, dx=0, dy=0):
-        return ((z + dz + 8) % 8, (c + dc) % 2, (x + dx + 4) % 4, (y + dy + 4) % 4)
+        return ((z + dz + 8) & 7, (c + dc) & 1, (x + dx + 4) & 3, (y + dy + 4) & 3)
 
     def slot(dx, dy):
-        return ((x + dx + 4) % 4) * 4 + (y + dy + 4) % 4
+        return ((x + dx + 4) & 3) * 4 + ((y + dy + 4) & 3)
 
     def remote(src, dst, ssem, rsem, dev):
         return pltpu.make_async_remote_copy(
@@ -82,16 +84,16 @@
         pltpu.make_async_copy(w_hbm, wbuf.at[z * 2 + c], l_sem.at[1]),
         pltpu.make_async_copy(so_hbm, so, l_sem.at[2]),
         pltpu.make_async_copy(gt_hbm, gt, l_sem.at[3]),
-        pltpu.make_async_copy(bin_hbm, stage.at[0], l_sem.at[4]),
-        pltpu.make_async_copy(cin_hbm, stage.at[1], l_sem.at[5]),
+        pltpu.make_async_copy(bin_hbm, wts.at[:, 0:128], l_sem.at[4]),
+        pltpu.make_async_copy(cin_hbm, wts.at[:, 128:256], l_sem.at[5]),
     ]
     for load in loads:
         load.start()
     barrier = pltpu.get_barrier_semaphore()
 
     def greet(k, carry_):
-        other = (head + k) % 16
-        pl.semaphore_signal(barrier, inc=1, device_id=(z, c, other // 4, other % 4), device_id_type=MESH)
+        other = (head + k) & 15
+        pl.semaphore_signal(barrier, inc=1, device_id=(z, c, other >> 2, other & 3), device_id_type=MESH)
         return carry_
 
     lax.fori_loop(1, 16, greet, 0)
@@ -124,12 +126,12 @@
         sign = 1 if d == 0 else -1
         far = (k // 2 if k < 6 else 3) + (1 if got else 0)
         half = k % 2 if k < 6 else d
-        here = ((z - sign * far + 8) % 8) * 2 + c
+        here = ((z - sign * far + 8) & 7) * 2 + c
         piece = wbuf.at[here, pl.ds(half * 128, 128)]
         return remote(piece, piece, w_ssem.at[d, k], w_rsem.at[d, k], at(dz=sign))
 
     def b_copy(k, got):
-        here = ((z + k) % 8) * 2 + ((c + 1) % 2 if got else c)
+        here = ((z + k) & 7) * 2 + ((1 - c) if got else c)
         return remote(wbuf.at[here], wbuf.at[here], b_ssem.at[k], b_rsem.at[k], at(dc=1))
 
     @scoped
@@ -149,10 +151,10 @@
             b_copy(4, False).start()
 
     def row_copy(slots, ssem, rsem, k, got):
-        other = (head + k) % 16
-        source = (head + 16 - k) % 16
+        other = (head + k) & 15
+        source = (head + 16 - k) & 15
         here = source if got else head
-        return remote(slots.at[here], slots.at[here], ssem.at[k], rsem.at[k], (z, c, other // 4, other % 4))
+        return remote(slots.at[here], slots.at[here], ssem.at[k], rsem.at[k], (z, c, other >> 2, other & 3))
 
     def row_send(slots, ssem, rsem):
         def one(k, carry_):
@@ -247,7 +249,7 @@
 
             @pl.loop(0, 4)
             def _(r, which=which, sel=sel):
-                conv[...] = stage[which, pl.ds(pl.multiple_of(r * 2048, 2048), 2048), :].astype(F32)
+                conv[...] = wts[pl.ds(pl.multiple_of(r * 2048, 2048), 2048), which * 128 : which * 128 + 128].astype(F32)
                 sel[pl.ds(pl.multiple_of(r * 256, 256), 256), :] = conv[pl.ds(group, 256, stride=8), :].astype(BF16)
 
         ct[...] = csel[...].astype(F32).T.astype(BF16)
@@ -266,7 +268,7 @@
             for h in range(8):
                 gap = cum_s[h : h + 1, rows] - columns[:, CUM + h : CUM + h + 1]
                 decayed = jnp.where(keep_upper, scores * jnp.exp(jnp.minimum(gap, 0.0)), 0.0)
-                wts[k, h] = decayed.astype(BF16)
+                wts[pl.ds(pl.multiple_of(k * 2048 + h * 256, 256), 256), :] = decayed.astype(BF16)
 
     @scoped
     def normalize(mean):
@@ -279,125 +281,152 @@
             normed = gated[rows, :] * col[rows, :][:, 0:1] * nw
             normt[:, rows] = normed.T.astype(BF16)
 
-    def pair_slots(p):
-        (ex, ey), (ox, oy) = PAIRS[p]
-        return slot(ex, ey), slot(ox, oy)
-
-    def mine_and_other(p):
-        first, second = pair_slots(p)
-        same = (y + PAIRS[p][0][1] + 4 + c) % 2 == 0
-        return jnp.where(same, first, second), jnp.where(same, second, first)
-
-    def give_copy(p):
-        return remote(gout.at[p], gin.at[p], h_ssem.at[p], h_rsem.at[p], at(dc=1))
-
-    @scoped
-    def weight_part(p):
-        mine, other = mine_and_other(p)
-
+    owners = [slot(*block) for block in BLOCKS]
+
+    def give_copy(q):
+        return remote(gkeep.at[q], gin.at[q], h_ssem.at[q], h_rsem.at[q], at(dc=1))
+
+    def kept(q):
+        return (owners[q] & 1) == c if q < SPLIT else c == 0
+
+    def given(q):
+        return (owners[q] & 1) != c if q < SPLIT else c == 1
+
+    @scoped
+    def weight_part(group):
         @pl.loop(0, 4)
         def _(r):
             rows = rows128(r)
             lhs = normt[rows, :]
-            gout[p, rows, :] = jnp.dot(lhs, abuf[other], preferred_element_type=F32).astype(BF16)
-            gkeep[p, rows, :] = jnp.dot(lhs, abuf[mine], preferred_element_type=F32).astype(BF16)
-
-        give_copy(p).start()
-
-    @scoped
-    def grad_part(p):
-        first, second = pair_slots(p)
-
+            for q in group:
+                gkeep[q, rows, :] = jnp.dot(lhs, abuf[owners[q]], preferred_element_type=F32).astype(BF16)
+
+        for q in group:
+
+            @pl.when(given(q))
+            def _():
+                give_copy(q).start()
+
+    @scoped
+    def grad_part(group):
         @pl.loop(0, 4)
         def _(r):
             rows = pl.ds(pl.multiple_of(r * 256, 256), 256)
-            add = jnp.dot(abuf[first, rows, :], wbuf[first], preferred_element_type=F32)
-            add = add + jnp.dot(abuf[second, rows, :], wbuf[second], preferred_element_type=F32)
-            if p == 0:
-                ng[rows, :] = add
-            else:
-                ng[rows, :] += add
-
-    def among(i, values):
-        found = values[0]
-        for q in range(1, len(values)):
-            found = jnp.where(i == q, values[q], found)
-        return found
-
-    roots = [mine_and_other(p)[0] // 2 for p in range(8)]
-
-    def r_copy(p, i, way):
-        piece = pl.ds(i * 256, 256)
-        dev = ((z + jnp.where(way == 0, 1, 7)) % 8, c, x, y)
-        return remote(gkeep.at[p, piece], fromz.at[way, p, piece], r_ssem.at[p, i], r_rsem.at[p, i, way], dev)
-
-    @scoped
-    def combine(p):
-        give_copy(p).wait_recv()
-        gkeep[p] = (gkeep[p].astype(F32) + gin[p].astype(F32)).astype(BF16)
-
-    def rs_level(p, lev):
-        rel = (z - among(p, roots) + 8) % 8
+            add = None if 0 in group else ng[rows, :]
+            for q in group:
+                more = jnp.dot(abuf[owners[q], rows, :], wbuf[owners[q]], preferred_element_type=F32)
+                add = more if add is None else add + more
+            ng[rows, :] = add
+
+    def r_copy(q, i, n, way, last=None):
+        size = 256 // CUTS[q]
+        piece = pl.ds(pl.multiple_of(i * 256 + n * size, size), size)
+        dev = ((z + jnp.where(way == 0, 1, 7)) & 7, c, x, y)
+        dst = fromz.at[q, piece] if last is None else rootb.at[last, piece]
+        return remote(gkeep.at[q, piece], dst, r_ssem.at[q, i, n], r_rsem.at[q, i, way, n], dev)
+
+    def cuts(q, fn):
+        if CUTS[q] == 1:
+            fn(0)
+        else:
+            pl.loop(0, CUTS[q])(fn)
+
+    def add_rows(q, row, n, term):
+        step = min(n, 64)
+
+        @pl.loop(0, n // step)
+        def _(r):
+            rows = pl.ds(pl.multiple_of(row + r * step, step), step)
+            gkeep[q, rows, :] = (gkeep[q, rows, :].astype(F32) + term[q, rows, :].astype(F32)).astype(BF16)
+
+    def rs_level(q, lev):
+        owner = owners[q]
+        rel = (z - (owner >> 1) + 8) & 7
+        which = owner & 1
+        if lev == 0:
+            give_copy(q).wait_recv()
+            add_rows(q, 0, 512, gin)
+        if lev == 4:
+
+            @pl.when(rel == 0)
+            def _():
+                for i in (0, 1):
+
+                    @functools.partial(cuts, q)
+                    def _(n):
+                        r_copy(q, i, n, 0).wait_recv()
+                        r_copy(q, i, n, 1, which).wait_recv()
+
+                @pl.loop(0, 4)
+                def _(r):
+                    rows = rows128(r)
+                    total = (
+                        gkeep[q, rows, :].astype(F32)
+                        + fromz[q, rows, :].astype(F32)
+                        + rootb[which, rows, :].astype(F32)
+                    )
+                    gw[which, :, rows] = total.T * (1.0 / math.sqrt(16384.0))
+
+            return
         for i in (0, 1):
-            piece = pl.ds(i * 256, 256)
-            way = jnp.where(rel >= 4 + i, 0, 1)
-            level = jnp.where(rel >= 4 + i, rel - (4 + i), (3 + i) - rel)
-
-            @pl.when((rel != 0) & (level == lev))
+            high, low = 4 + i + lev, 3 + i - lev
+            here = rel == high if high <= 7 else None
+            if low >= 1:
+                here = (rel == low) if here is None else here | (rel == low)
+            if here is None:
+                continue
+
+            @pl.when(here)
             def _():
-                copy = r_copy(p, i, way)
-
-                @pl.when(lev > 0)
+                way = jnp.where(rel >= 4 + i, 0, 1)
+
+                @functools.partial(cuts, q)
+                def _(n):
+                    if lev:
+                        r_copy(q, i, n, way).wait_recv()
+                        size = 256 // CUTS[q]
+                        add_rows(q, i * 256 + n * size, size, fromz)
+
+                    @pl.when(rel == 1)
+                    def _():
+                        r_copy(q, i, n, way, which).start()
+
+                    @pl.when(rel != 1)
+                    def _():
+                        r_copy(q, i, n, way).start()
+
+    @scoped
+    def rs_stage(*steps):
+        for group, lev in steps:
+            for q in group:
+
+                @pl.when(kept(q))
                 def _():
-                    copy.wait_recv()
-                    gkeep[p, piece, :] = (
-                        gkeep[p, piece, :].astype(F32) + fromz[way, p, piece, :].astype(F32)
-                    ).astype(BF16)
-
-                copy.start()
-
-        @pl.when((rel == 0) & (lev == 4))
-        def _():
-            for i in (0, 1):
-                piece = pl.ds(i * 256, 256)
-                r_copy(p, i, 0).wait_recv()
-                r_copy(p, i, 1).wait_recv()
-                total = (
-                    gkeep[p, piece, :].astype(F32)
-                    + fromz[0, p, piece, :].astype(F32)
-                    + fromz[1, p, piece, :].astype(F32)
-                )
-                gw[:, i * 256 : i * 256 + 256] = total.T * (1.0 / math.sqrt(16384.0))
-
-    @scoped
-    def rs_stage(*steps):
-        for p, lev in steps:
-            if lev == 0:
-                combine(p)
-        ps, levs = [p for p, _ in steps], [lev for _, lev in steps]
-
-        def one(i, carry_):
-            rs_level(among(i, ps), among(i, levs))
-            return carry_
-
-        lax.fori_loop(0, len(steps), one, 0)
+                    rs_level(q, lev)
+
+    handed = owners[SPLIT] == 2 * z + 1
+    for q in range(SPLIT + 1, 16):
+        handed = handed | (owners[q] == 2 * z + 1)
+
+    def out_copy():
+        return remote(gw.at[1], gw.at[1], o_ssem.at[0], o_rsem.at[0], (z, 1, x, y))
 
     def hop_copy(buf, ssem, rsem, way, d, got, *rest):
-        source = z + (d if got else d - 1) if way == 1 else (z + 8 - (d if got else d - 1)) % 8
+        source = z + (d if got else d - 1) if way == 1 else ((z + 8 - (d if got else d - 1)) & 7)
         here = jnp.minimum(source, 7)
         piece = buf.at[(here, *rest)]
         index = (way, d - 1)
         if rest:
-            index = (way, d - 1, rest[0].start // 64)
-        return remote(piece, piece, ssem.at[index], rsem.at[index], ((z + (1 if way == 0 else 7)) % 8, 1, x, y))
+            index = (way, d - 1, rest[0].start // 16)
+        return remote(piece, piece, ssem.at[index], rsem.at[index], ((z + (1 if way == 0 else 7)) & 7, 1, x, y))
 
     def hop_valid(way, d, got):
         if way == 1:
             return (z + d <= 7) if got else ((z > 0) & (z + d - 1 <= 7))
-        return (z + 8 - (d if got else d - 1)) % 8 >= 5
+        return ((z + 8 - (d if got else d - 1)) & 7) >= 5
 
     WAYS = ((1, 1), (0, 1), (1, 2), (0, 2), (1, 3), (0, 3), (1, 4))
-    HALVES = (pl.ds(0, 64), pl.ds(64, 64))
+    HALVES = [pl.ds(16 * i, 16) for i in range(8)]
 
     def decay_copy(way, d, got):
         return hop_copy(dall, e_ssem, e_rsem, way, d, got)
@@ -487,58 +516,61 @@
     decay_hop(0)
     a_wait(*every(1))
     a_send((1, 2), (1, 4), (2, 2), (2, 4))
-    weight_part(0)
+    weight_part(G0)
     w_event(4)
-    weight_part(1)
     w_event(5)
     decay_hop(1)
     a_wait((0, 2), (3, 2), (1, 3), (2, 3))
-    a_send(*every(5))
-    rs_stage((0, 0), (1, 0))
+    a_send((2, 5), (3, 5), (1, 6))
+    rs_stage((G0A, 0))
     w_event(6)
     decay_hop(2)
     a_wait((0, 3), (1, 2), (2, 2), (3, 3))
-    a_send(*every(6))
-    weight_part(2)
+    a_send((0, 6), (2, 6), (3, 6))
+    rs_stage((G0B, 0))
+    weight_part(G1)
     with jax.named_scope("b_wait"):
         for k in range(8):
             b_copy(k, True).wait_recv()
+    grad_part(range(0, 4))
+    rs_stage((G0A, 1), (G1, 0))
+    a_wait(*every(4))
+    a_send((0, 7), (1, 7), (2, 7), (3, 7), (0, 5), (1, 5), (0, 9), (1, 9))
+    grad_part(range(4, 8))
     decay_hop(3)
-    grad_part(0)
-    grad_part(1)
-    grad_part(2)
+    rs_stage((G0B, 1))
+    weight_part(G2)
+    rs_stage((G0A, 2))
+    grad_part(G2)
+    a_wait((0, 6), (1, 6), (0, 7), (1, 7), (2, 5), (3, 5))
+    a_send((2, 8), (3, 8))
+    rs_stage((G1, 1), (G2, 0))
+    weight_part(G3)
     decay_hop(4)
-    a_wait(*every(4))
-    a_send(*every(7))
-    rs_stage((0, 1), (1, 1), (2, 0))
-    weight_part(3)
-    grad_part(3)
-    weight_part(4)
-    grad_part(4)
-    a_wait(*every(5))
-    a_send(*every(8))
-    rs_stage((0, 2), (1, 2), (2, 1), (3, 0), (4, 0))
-    a_wait(*every(6))
-    weight_part(5)
-    grad_part(5)
-    a_wait(*every(7))
-    grad_part(6)
-    weight_part(6)
-    rs_stage((0, 3), (1, 3), (2, 2), (3, 1), (4, 1), (5, 0))
+    rs_stage((G0B, 2))
+    a_wait((0, 5), (1, 5), (2, 6), (3, 6))
+    a_send((0, 8), (1, 8))
+    grad_part(G3)
+    rs_stage((G0A, 3), (G3, 0))
+    a_wait((0, 9), (1, 9), (2, 7), (3, 7))
+    grad_part(range(13, 15))
+    rs_stage((G1, 2), (G2, 1))
     a_wait(*every(8))
-    grad_part(7)
 
     with jax.named_scope("weighted"):
-
-        @pl.loop(0, 8)
+        last = owners[15]
+
+        @pl.loop(0, 4)
         def _(r):
-            rows = rows128(r)
-            term = nw_ref[...] * ng[rows, :] * gated[rows, :]
+            rows = pl.ds(pl.multiple_of(r * 256, 256), 256)
+            done = ng[rows, :] + jnp.dot(abuf[last, rows, :], wbuf[last], preferred_element_type=F32)
+            ng[rows, :] = done
+            term = nw_ref[...] * done * gated[rows, :]
             wds[head, :, rows] = jnp.sum(fold_lanes(term).T, axis=0, keepdims=True)
 
     row_send(wds, d_ssem, d_rsem)
-    weight_part(7)
-    rs_stage((6, 0))
+    weight_part(G4)
+    rs_stage((G4, 0), (G0B, 3), (G3, 1), (G1, 3), (G2, 2))
 
     @pl.when(c == 1)
     def _():
@@ -582,7 +614,25 @@
         s0buf[0] = summary().astype(BF16)
         s0_copy().start()
 
-    rs_stage((7, 0))
+    @scoped
+    def within_all():
+        low = lax.broadcasted_iota(jnp.int32, (BLK, 128), 1) < 64
+
+        @pl.loop(0, 4)
+        def _(k):
+            rows = pl.ds(pl.multiple_of(k * BLK, BLK), BLK)
+            for hp in range(4):
+                cols = slice(hp * 128, hp * 128 + 128)
+                g = gs[rows, cols]
+                zero = jnp.zeros_like(g)
+                even, odd = (wts[pl.ds(pl.multiple_of(k * 2048 + h * 256, 256), 256), :] for h in (2 * hp, 2 * hp + 1))
+                ng[rows, cols] = jnp.dot(even, jnp.where(low, g, zero), preferred_element_type=F32) + jnp.dot(
+                    odd, jnp.where(low, zero, g), preferred_element_type=F32
+                )
+
+    rs_stage((G4, 1), (G3, 2))
+    within_all()
+    rs_stage((G2, 3))
 
     @pl.when(c == 1)
     def _():
@@ -591,23 +641,6 @@
             s0_copy().wait_recv()
         sall[z] = (s0buf[1].astype(F32) + own).astype(BF16)
         state_hop(0)
-
-    @scoped
-    def within_all():
-        low = lax.broadcasted_iota(jnp.int32, (BLK, 128), 1) < 64
-
-        @pl.loop(0, 4)
-        def _(k):
-            rows = pl.ds(pl.multiple_of(k * BLK, BLK), BLK)
-            for hp in range(4):
-                cols = slice(hp * 128, hp * 128 + 128)
-                g = gs[rows, cols]
-                zero = jnp.zeros_like(g)
-                ng[rows, cols] = jnp.dot(
-                    wts[k, 2 * hp], jnp.where(low, g, zero), preferred_element_type=F32
-                ) + jnp.dot(wts[k, 2 * hp + 1], jnp.where(low, zero, g), preferred_element_type=F32)
-
-    within_all()
 
     def take(k):
         @pl.when(z + k <= 7)
@@ -624,12 +657,9 @@
             if d < 4:
                 take(8 - d)
 
-    hop_and_take(1)
-    rs_stage((0, 4), (1, 4), (2, 3), (3, 2), (4, 2), (5, 1), (6, 1), (7, 1))
-    hop_and_take(2)
     with jax.named_scope("sends_1"):
         for d in range(4):
-            for k in range(9):
+            for k in range(len(ITEMS[d])):
                 a_copy(d, k, False).wait_send()
         for d in (0, 1):
             for k in range(7):
@@ -637,9 +667,9 @@
         for k in range(8):
             b_copy(k, False).wait_send()
         row_done(sqs, g_ssem, g_rsem)
-    hop_and_take(3)
-    rs_stage((2, 4), (3, 3), (4, 3), (5, 2), (6, 2), (7, 2))
-    hop_and_take(4)
+        row_done(wds, d_ssem, d_rsem)
+    for d in (1, 2, 3, 4):
+        hop_and_take(d)
 
     @pl.when(c == 1)
     def _():
@@ -647,7 +677,12 @@
         carry[0] = (own + d0buf[0] * acc[...]).astype(BF16)
         core_copy().start()
 
-    rs_stage((3, 4), (4, 4), (5, 3), (6, 3), (7, 3))
+    rs_stage((G4, 2), (G3, 3), (G0A, 4), (G0B, 4))
+    rs_stage((G4, 3), (G1, 4), (G2, 4), (G3, 4), (G4, 4))
+
+    @pl.when((c == 0) & handed)
+    def _():
+        out_copy().start()
 
     @pl.when(c == 0)
     def _():
@@ -662,6 +697,7 @@
             skw = jnp.where(lane512 == h, skip_ref[0, h], skw)
         gate_out.wait()
         state = acc[...]
+        x_outs = []
         for k in (3, 2, 1, 0):
             rows = slice(k * BLK, (k + 1) * BLK)
             across = jnp.dot(bsel[rows, :], state.astype(BF16), preferred_element_type=F32)
@@ -669,39 +705,73 @@
                 state = st[k] + ends[k] * state
             out = tsw[rows, :] * (ng[rows, :] + etw[rows, :] * across) + skw * gs[rows, :].astype(F32)
             so[rows, :] = out.astype(BF16)
-        x_out = pltpu.make_async_copy(so, gx_hbm, l_sem.at[2])
-        x_out.start()
-
-    rs_stage((5, 4), (6, 4), (7, 4))
-    gw_out = pltpu.make_async_copy(gw, gw_hbm, l_sem.at[1])
+            x_out = pltpu.make_async_copy(so.at[rows], gx_hbm.at[rows], l_sem.at[2 + k])
+            x_out.start()
+            x_outs.append(x_out)
+
+    @pl.when((c == 1) & handed)
+    def _():
+        with jax.named_scope("out_wait"):
+            out_copy().wait_recv()
+
+    gw_out = pltpu.make_async_copy(gw.at[c], gw_hbm, l_sem.at[1])
     gw_out.start()
 
     with jax.named_scope("sends_2"):
-        row_done(wds, d_ssem, d_rsem)
-
-        def one(p, carry_):
-            @pl.when((z - among(p, roots) + 8) % 8 != 0)
-            def _():
-                for i in (0, 1):
-                    r_copy(p, i, 0).wait_send()
-
-            give_copy(p).wait_send()
-            return carry_
-
-        lax.fori_loop(0, 8, one, 0)
 
         @pl.when(c == 0)
         def _():
             d0_copy().wait_send()
             s0_copy().wait_send()
 
+            @pl.when(handed)
+            def _():
+                out_copy().wait_send()
+
         @pl.when(c == 1)
         def _():
             core_copy().wait_send()
             hops_done()
 
+        for q in range(16):
+
+            @pl.when(given(q))
+            def _():
+                give_copy(q).wait_send()
+
+            @pl.when(kept(q) & (((z - (owners[q] >> 1) + 8) & 7) != 0))
+            def _():
+                for i in (0, 1):
+
+                    @functools.partial(cuts, q)
+                    def _(n):
+                        r_copy(q, i, n, 0).wait_send()
+
         gw_out.wait()
-        x_out.wait()
+        for x_out in x_outs:
+            x_out.wait()
+
+
+def move(*refs):
+    ins, outs, bufs, (in_sem, out_sem) = refs[:3], refs[3:6], refs[6:9], refs[9:]
+    steps = []
+    for k in range(3):
+        n = ins[k].shape[0] // 4
+        for r in range(4):
+            rows = pl.ds(r * n, n)
+            steps.append(
+                (
+                    pltpu.make_async_copy(ins[k].at[rows], bufs[k].at[rows], in_sem.at[k, r]),
+                    pltpu.make_async_copy(bufs[k].at[rows], outs[k].at[rows], out_sem.at[k, r]),
+                )
+            )
+    for first, _ in steps:
+        first.start()
+    for first, second in steps:
+        first.wait()
+        second.start()
+    for _, second in steps:
+        second.wait()
 
 
 def on_device(a, w, so, gt, nw, ts, ld, bin_, cin, skip):
@@ -709,7 +779,7 @@
     vmem = pl.BlockSpec(memory_space=pltpu.VMEM)
     smem = pl.BlockSpec(memory_space=pltpu.SMEM)
     V, D = pltpu.VMEM, pltpu.SemaphoreType.DMA
-    return pl.pallas_call(
+    results = pl.pallas_call(
         kernel,
         out_shape=(
             jax.ShapeDtypeStruct((1024, 512), BF16),
@@ -721,24 +791,34 @@
         scratch_shapes=[
             V((16, 1024, 256), BF16), V((16, 256, 512), BF16), V((1024, 512), BF16), V((1024, 512), BF16),
             V((1024, 512), F32), V((1024, 512), F32), V((1024, 512), F32), V((1024, 512), F32),
-            V((1024, 512), F32), V((1024, 512), F32), V((1024, 512), F32), V((4, 8, 256, 256), BF16),
-            V((8, 512, 256), BF16), V((8, 512, 256), BF16), V((8, 512, 256), BF16), V((2, 8, 512, 256), BF16),
-            V((512, 1024), BF16), V((2, 8192, 128), BF16), V((2048, 128), F32), V((1024, 128), BF16),
+            V((1024, 512), F32), V((1024, 512), F32), V((1024, 512), F32), V((8192, 256), BF16),
+            V((16, 512, 256), BF16), V((16, 512, 256), BF16), V((16, 512, 256), BF16), V((2, 512, 256), BF16),
+            V((512, 1024), BF16), V((2048, 128), F32), V((1024, 128), BF16),
             V((1024, 128), BF16), V((128, 1024), BF16), V((1024, 128), F32), V((8, 1024), F32), V((1024, 128), F32),
             V((16, 1, 1024), F32), V((16, 1, 1024), F32), V((4, 128, 512), F32), V((128, 512), F32),
             V((2, 128, 512), BF16), V((2, 1, 512), F32), V((8, 128, 512), BF16), V((8, 1, 512), F32),
-            V((8, 1, 512), F32), V((2, 128, 512), BF16), V((256, 512), F32),
-            D((4, 9)), D((4, 9)), D((2, 7)), D((2, 7)), D((8,)), D((8,)), D((8, 2)), D((8, 2, 2)), D((16,)), D((16,)),
-            D((8,)), D((8,)), D((16,)), D((16,)), D((2,)), D((2,)), D((1,)), D((1,)), D((2, 4, 2)), D((2, 4, 2)),
-            D((2, 4)), D((2, 4)), D((6,)),
+            V((8, 1, 512), F32), V((2, 128, 512), BF16), V((2, 256, 512), F32),
+            D((4, 10)), D((4, 10)), D((2, 7)), D((2, 7)), D((8,)), D((8,)), D((16, 2, 4)), D((16, 2, 2, 4)), D((16,)), D((16,)),
+            D((16,)), D((16,)), D((16,)), D((16,)), D((2,)), D((2,)), D((1,)), D((1,)), D((2, 4, 8)), D((2, 4, 8)),
+            D((2, 4)), D((2, 4)), D((1,)), D((1,)), D((6,)),
         ],
         compiler_params=pltpu.CompilerParams(
-            collective_id=0, has_side_effects=True, vmem_limit_bytes=67043328
+            collective_id=0, has_side_effects=True, vmem_limit_bytes=59768832
         ),
         name="mixer_backward",
     )(
         a, w, so, gt, nw.reshape(1, 512), ts, ld, bin_.reshape(8192, 128), cin.reshape(8192, 128), skip.reshape(1, 8)
     )
+    V, D = pltpu.VMEM, pltpu.SemaphoreType.DMA
+    return pl.pallas_call(
+        move,
+        out_shape=[jax.ShapeDtypeStruct(r.shape, r.dtype) for r in results],
+        in_specs=[any_] * 3,
+        out_specs=[any_] * 3,
+        scratch_shapes=[V(r.shape, r.dtype) for r in results] + [D((3, 4)), D((3, 4))],
+        compiler_params=pltpu.CompilerParams(vmem_limit_bytes=62914560),
+        name="move",
+    )(*results)
 
 
 def solution(mesh):

time: 99 us -> 91.8 us (0.927)
  the two profiles are of different devices: /device:TPU:45 before, /device:TPU:21 now
where the time goes in v3:
time: 91.8 us; the launch traced here: 90.4 us
  Pallas kernels  89.6 us (98%)
    pallas_call x1, Pallas kernels, on_device(): pl.pallas_call(kernel, out_shape=(jax.ShapeDtypeStruct((1024, 512), BF16)...  87 us
    pallas_call x1, Pallas kernels, on_device(): pl.pallas_call(move, out_shape=[jax.ShapeDtypeStruct(r.shape, r.dtype) fo...  2.63 us

profile of v3, /device:TPU:21, one launch (start us, length us, event | category | flops | bytes accessed | tf_op | source)
XLA Modules:
  0.0 90.4 jit_solution(13524629009881530902)
XLA Ops:
  0.6 87.0 %mixer_backward.1 = (bf16[1024,512]{1,0:T(8,128)(2,1)}, bf16[1024,512]{1,0:T(8,128)(2,1)}, f32[256,512]{1,0:T(8,128)}) custom-call(bf16[1024,256]{1,0:T(8,128)(2,1)} %a_hbm.1, bf16[256,512]{1,0:T(8,128)(2,1)} %w_hbm.1, bf16[1024,512]{1,0:T(8,128)(2,1)} %so_hbm.1, bf16[1024,512]{1,0:T(8,128)(2,1)} %gt_hbm.1, f32[1,512]{1,0:T(1,128)} %bitcast.6, ...), custom_call_target="tpu_custom_call" | custom-call | tf_op jit(solution)/shard_map/mixer_backward/pallas_call | solution.py:782
  87.6 2.6 %move.1 = (bf16[1024,512]{1,0:T(8,128)(2,1)}, bf16[1024,512]{1,0:T(8,128)(2,1)}, f32[256,512]{1,0:T(8,128)}) custom-call(bf16[1024,512]{1,0:T(8,128)(2,1)} %get-tuple-element.6.refs_0_, bf16[1024,512]{1,0:T(8,128)(2,1)} %get-tuple-element.7.refs_1_, f32[256,512]{1,0:T(8,128)} %get-tuple-element.8.refs_2_), custom_call_target="tpu_custom_call" | custom-call | tf_op jit(solution)/shard_map/move/pallas_call | solution.py:813

commit v4 on v3

--- a/solution.py
+++ b/solution.py
@@ -22,6 +22,18 @@
     ((0, 0, B), (0, 0, A), (0, -1, A), (1, 0, A), (-1, 0, A), (2, 0, A), (1, -1, A0), (-1, -1, A0), (2, -1, A0)),
     ((0, 0, B), (0, 0, A), (0, 1, B), (1, 0, A), (-1, 0, A), (2, 0, A), (1, 1, A1), (-1, 1, A1), (2, 1, A1)),
 )
+EVENTS = (
+    (((0, 0), (1, 0), (2, 0), (3, 0)), 2),
+    (((0, 1), (1, 1), (2, 1), (3, 1)), 2),
+    (((0, 2), (3, 2), (1, 3), (2, 3)), 2),
+    (((0, 3), (1, 2), (2, 2), (3, 3)), 2),
+    (((0, 4), (1, 4), (2, 4), (3, 4)), 2),
+    (((0, 6), (1, 6), (0, 7), (1, 7), (2, 5), (3, 5)), 2),
+    (((0, 5), (1, 5), (2, 6), (3, 6)), 1),
+    (((0, 9), (1, 9), (2, 7), (3, 7)), 1),
+    (((0, 8), (1, 8), (2, 8), (3, 8)), 1),
+)
+EVENT_OF = {flow: e for e, (flows, _) in enumerate(EVENTS) for flow in flows}
 BLOCKS = (
     (0, 0), (0, 1), (1, 0), (0, -1), (-1, 0),
     (2, 0), (0, 2), (1, 1),
@@ -61,8 +73,8 @@
     a_hbm, w_hbm, so_hbm, gt_hbm, nw_ref, ts_ref, ld_ref, bin_hbm, cin_hbm, skip_ref,
     gx_hbm, gg_hbm, gw_hbm,
     abuf, wbuf, so, gt, gated, silu, fgate, ng, ecw, etw, tsw, wts, gkeep, gin, fromz, rootb,
-    normt, conv, bsel, csel, ct, qt, cum_s, col, sqs, wds, st, acc, s0buf, d0buf, sall, dall, weight, carry, gw,
-    a_ssem, a_rsem, w_ssem, w_rsem, b_ssem, b_rsem, r_ssem, r_rsem, g_ssem, g_rsem, h_ssem, h_rsem,
+    normt, conv, bsel, csel, ct, qt, cum_s, col, sqs, wds, st, acc, s0buf, d0buf, schip, legs, mout, vout, decays, carry, gw,
+    a_ssem, a_rsem, w_ssem, w_rsem, b_rsem, r_ssem, r_rsem, g_ssem, g_rsem, h_rsem,
     d_ssem, d_rsem, s_ssem, s_rsem, c_ssem, c_rsem, m_ssem, m_rsem, e_ssem, e_rsem, o_ssem, o_rsem, l_sem,
 ):
     z, c, x, y = (lax.axis_index(n) for n in ("z", "c", "x", "y"))
@@ -104,84 +116,67 @@
         loads[1].wait()
         pl.semaphore_wait(barrier, 18)
 
-    def a_copy(d, k, got):
-        dx, dy, (row, n) = ITEMS[d][k]
-        sx, sy = STEP[d]
-        here = slot(dx - sx, dy - sy) if got else slot(dx, dy)
-        piece = abuf.at[here, pl.ds(row, n)]
-        return remote(piece, piece, a_ssem.at[d, k], a_rsem.at[d, k], at(dx=sx, dy=sy))
-
     def a_send(*flows):
         for d, k in flows:
-            a_copy(d, k, False).start()
-
-    @scoped
-    def a_wait(*flows):
-        for d, k in flows:
-            a_copy(d, k, True).wait_recv()
+            dx, dy, (row, n) = ITEMS[d][k]
+            sx, sy = STEP[d]
+            piece = abuf.at[slot(dx, dy), pl.ds(row, n)]
+            remote(piece, piece, a_ssem.at[0], a_rsem.at[EVENT_OF[d, k]], at(dx=sx, dy=sy)).start()
+
+    def whole(buf, n, sem):
+        part = buf.at[pl.ds(0, n)]
+        pltpu.make_async_copy(part, part, sem).wait()
+
+    @scoped
+    def a_wait(event):
+        whole(abuf, EVENTS[event][1], a_rsem.at[event])
 
     every = lambda k: [(d, k) for d in range(4)]
 
-    def w_copy(d, k, got):
+    def w_copy(d, k):
         sign = 1 if d == 0 else -1
-        far = (k // 2 if k < 6 else 3) + (1 if got else 0)
+        far = k // 2 if k < 6 else 3
         half = k % 2 if k < 6 else d
         here = ((z - sign * far + 8) & 7) * 2 + c
         piece = wbuf.at[here, pl.ds(half * 128, 128)]
-        return remote(piece, piece, w_ssem.at[d, k], w_rsem.at[d, k], at(dz=sign))
-
-    def b_copy(k, got):
-        here = ((z + k) & 7) * 2 + ((1 - c) if got else c)
-        return remote(wbuf.at[here], wbuf.at[here], b_ssem.at[k], b_rsem.at[k], at(dc=1))
+        return remote(piece, piece, w_ssem.at[0], w_rsem.at[k], at(dz=sign))
+
+    def b_copy(k):
+        here = ((z + k) & 7) * 2 + c
+        return remote(wbuf.at[here], wbuf.at[here], w_ssem.at[0], b_rsem.at[0], at(dc=1))
 
     @scoped
     def w_event(k):
-        for d in (0, 1):
-            w_copy(d, k, True).wait_recv()
-            if k < 4:
-                w_copy(d, k + 2, False).start()
+        whole(wbuf, 1, w_rsem.at[k])
+        if k < 4:
+            for d in (0, 1):
+                w_copy(d, k + 2).start()
         if k == 4:
-            w_copy(0, 6, False).start()
+            w_copy(0, 6).start()
         if k == 5:
-            w_copy(1, 6, False).start()
+            w_copy(1, 6).start()
         if k in (1, 3, 5):
-            b_copy((k + 1) // 2, False).start()
-            b_copy(8 - (k + 1) // 2, False).start()
+            b_copy((k + 1) // 2).start()
+            b_copy(8 - (k + 1) // 2).start()
         if k == 6:
-            b_copy(4, False).start()
-
-    def row_copy(slots, ssem, rsem, k, got):
-        other = (head + k) & 15
-        source = (head + 16 - k) & 15
-        here = source if got else head
-        return remote(slots.at[here], slots.at[here], ssem.at[k], rsem.at[k], (z, c, other >> 2, other & 3))
+            b_copy(4).start()
 
     def row_send(slots, ssem, rsem):
         def one(k, carry_):
-            row_copy(slots, ssem, rsem, k, False).start()
+            other = (head + k) & 15
+            here = slots.at[head]
+            remote(here, here, ssem.at[0], rsem.at[0], (z, c, other >> 2, other & 3)).start()
             return carry_
 
         lax.fori_loop(1, 16, one, 0)
 
     @scoped
-    def row_sum(slots, ssem, rsem):
-        def one(k, carry_):
-            copy = row_copy(slots, ssem, rsem, k, True)
-            copy.wait_recv()
-            return carry_
-
-        lax.fori_loop(1, 16, one, 0)
+    def row_sum(slots, rsem):
+        whole(slots, 15, rsem.at[0])
         total = slots[0]
         for k in range(1, 16):
             total = total + slots[k]
         return total
-
-    def row_done(slots, ssem, rsem):
-        def one(k, carry_):
-            row_copy(slots, ssem, rsem, k, False).wait_send()
-            return carry_
-
-        lax.fori_loop(1, 16, one, 0)
 
     def to_column(row):
         return jnp.broadcast_to(row, (128, row.shape[1])).T
@@ -284,7 +279,7 @@
     owners = [slot(*block) for block in BLOCKS]
 
     def give_copy(q):
-        return remote(gkeep.at[q], gin.at[q], h_ssem.at[q], h_rsem.at[q], at(dc=1))
+        return remote(gkeep.at[q], gin.at[q], r_ssem.at[q], h_rsem.at[q], at(dc=1))
 
     def kept(q):
         return (owners[q] & 1) == c if q < SPLIT else c == 0
@@ -322,8 +317,11 @@
         size = 256 // CUTS[q]
         piece = pl.ds(pl.multiple_of(i * 256 + n * size, size), size)
         dev = ((z + jnp.where(way == 0, 1, 7)) & 7, c, x, y)
-        dst = fromz.at[q, piece] if last is None else rootb.at[last, piece]
-        return remote(gkeep.at[q, piece], dst, r_ssem.at[q, i, n], r_rsem.at[q, i, way, n], dev)
+        src = gkeep.at[q, piece]
+        if last is not None:
+            return remote(src, rootb.at[last, piece], r_ssem.at[q], o_rsem.at[last], dev)
+        flow = 2 * q + i if q < 13 else 26 + (q - 13) * 8 + i * 4 + n
+        return remote(src, fromz.at[q, piece], r_ssem.at[q], r_rsem.at[flow], dev)
 
     def cuts(q, fn):
         if CUTS[q] == 1:
@@ -339,141 +337,229 @@
             rows = pl.ds(pl.multiple_of(row + r * step, step), step)
             gkeep[q, rows, :] = (gkeep[q, rows, :].astype(F32) + term[q, rows, :].astype(F32)).astype(BF16)
 
-    def rs_level(q, lev):
-        owner = owners[q]
-        rel = (z - (owner >> 1) + 8) & 7
-        which = owner & 1
-        if lev == 0:
-            give_copy(q).wait_recv()
-            add_rows(q, 0, 512, gin)
-        if lev == 4:
-
-            @pl.when(rel == 0)
-            def _():
-                for i in (0, 1):
-
-                    @functools.partial(cuts, q)
-                    def _(n):
-                        r_copy(q, i, n, 0).wait_recv()
-                        r_copy(q, i, n, 1, which).wait_recv()
-
-                @pl.loop(0, 4)
-                def _(r):
-                    rows = rows128(r)
-                    total = (
-                        gkeep[q, rows, :].astype(F32)
-                        + fromz[q, rows, :].astype(F32)
-                        + rootb[which, rows, :].astype(F32)
-                    )
-                    gw[which, :, rows] = total.T * (1.0 / math.sqrt(16384.0))
-
-            return
-        for i in (0, 1):
-            high, low = 4 + i + lev, 3 + i - lev
-            here = rel == high if high <= 7 else None
-            if low >= 1:
-                here = (rel == low) if here is None else here | (rel == low)
-            if here is None:
-                continue
-
-            @pl.when(here)
-            def _():
-                way = jnp.where(rel >= 4 + i, 0, 1)
+    def from_core(q):
+        give_copy(q).wait_recv()
+        add_rows(q, 0, 512, gin)
+
+    def rs_root(q):
+        which = owners[q] & 1
+
+        @pl.when(z == (owners[q] >> 1))
+        def _():
+            for i in (0, 1):
 
                 @functools.partial(cuts, q)
                 def _(n):
-                    if lev:
-                        r_copy(q, i, n, way).wait_recv()
-                        size = 256 // CUTS[q]
-                        add_rows(q, i * 256 + n * size, size, fromz)
-
-                    @pl.when(rel == 1)
-                    def _():
-                        r_copy(q, i, n, way, which).start()
-
-                    @pl.when(rel != 1)
-                    def _():
-                        r_copy(q, i, n, way).start()
+                    r_copy(q, i, n, 0).wait_recv()
+
+            there = rootb.at[which]
+            pltpu.make_async_copy(there, there, o_rsem.at[which]).wait()
+
+            @pl.loop(0, 4)
+            def _(r):
+                rows = rows128(r)
+                total = (
+                    gkeep[q, rows, :].astype(F32)
+                    + fromz[q, rows, :].astype(F32)
+                    + rootb[which, rows, :].astype(F32)
+                )
+                gw[which, :, rows] = total.T * (1.0 / math.sqrt(16384.0))
+
+    def rs_piece(q, i, n, lev):
+        rel = (z - (owners[q] >> 1) + 8) & 7
+        high, low = 4 + i + lev, 3 + i - lev
+        here = rel == high if high <= 7 else None
+        if low >= 1:
+            here = (rel == low) if here is None else here | (rel == low)
+        if here is None:
+            return
+
+        @pl.when(here)
+        def _():
+            way = jnp.where(rel >= 4 + i, 0, 1)
+            if lev:
+                r_copy(q, i, n, way).wait_recv()
+                size = 256 // CUTS[q]
+                add_rows(q, i * 256 + n * size, size, fromz)
+
+            @pl.when(rel == 1)
+            def _():
+                r_copy(q, i, n, way, owners[q] & 1).start()
+
+            @pl.when(rel != 1)
+            def _():
+                r_copy(q, i, n, way).start()
 
     @scoped
     def rs_stage(*steps):
         for group, lev in steps:
+            if group == G4:
+
+                @pl.when(c == 0)
+                def _():
+                    if lev == 4:
+                        for q in group:
+                            rs_root(q)
+                        return
+                    if lev == 0:
+                        for q in group:
+                            from_core(q)
+
+                    @pl.loop(0, 4)
+                    def _(n):
+                        for i in (0, 1):
+                            for q in group:
+                                rs_piece(q, i, n, lev)
+
+                continue
             for q in group:
 
                 @pl.when(kept(q))
                 def _():
-                    rs_level(q, lev)
+                    if lev == 4:
+                        rs_root(q)
+                        return
+                    if lev == 0:
+                        from_core(q)
+                    for i in (0, 1):
+                        rs_piece(q, i, 0, lev)
 
     handed = owners[SPLIT] == 2 * z + 1
     for q in range(SPLIT + 1, 16):
         handed = handed | (owners[q] == 2 * z + 1)
 
     def out_copy():
-        return remote(gw.at[1], gw.at[1], o_ssem.at[0], o_rsem.at[0], (z, 1, x, y))
-
-    def hop_copy(buf, ssem, rsem, way, d, got, *rest):
-        source = z + (d if got else d - 1) if way == 1 else ((z + 8 - (d if got else d - 1)) & 7)
-        here = jnp.minimum(source, 7)
-        piece = buf.at[(here, *rest)]
-        index = (way, d - 1)
-        if rest:
-            index = (way, d - 1, rest[0].start // 16)
-        return remote(piece, piece, ssem.at[index], rsem.at[index], ((z + (1 if way == 0 else 7)) & 7, 1, x, y))
-
-    def hop_valid(way, d, got):
-        if way == 1:
-            return (z + d <= 7) if got else ((z > 0) & (z + d - 1 <= 7))
-        return ((z + 8 - (d if got else d - 1)) & 7) >= 5
-
-    WAYS = ((1, 1), (0, 1), (1, 2), (0, 2), (1, 3), (0, 3), (1, 4))
-    HALVES = [pl.ds(16 * i, 16) for i in range(8)]
-
-    def decay_copy(way, d, got):
-        return hop_copy(dall, e_ssem, e_rsem, way, d, got)
-
-    def state_copy(way, d, got, half):
-        return hop_copy(sall, m_ssem, m_rsem, way, d, got, half)
+        return remote(gw.at[1], gw_hbm, o_ssem.at[0], o_rsem.at[2], (z, 1, x, y))
+
+    QUARTERS = [pl.ds(32 * i, 32) for i in range(4)]
+    X, V, R = range(3)
+
+    def leg(src, kind, q, dz):
+        return remote(
+            src.at[QUARTERS[q]], legs.at[kind, QUARTERS[q]], m_ssem.at[kind], m_rsem.at[kind, q], at(dz=dz)
+        )
+
+    def leg_wait(kind, q):
+        part = legs.at[kind, QUARTERS[q]]
+        pltpu.make_async_copy(part, part, m_rsem.at[kind, q]).wait()
 
     def decay_hop(d):
-        @pl.when(c == 1)
-        def _():
-            for way in (1, 0):
-                if d and (way, d) in WAYS:
-
-                    @pl.when(hop_valid(way, d, True))
-                    def _():
-                        decay_copy(way, d, True).wait_recv()
-
-                if (way, d + 1) in WAYS:
-
-                    @pl.when(hop_valid(way, d + 1, False))
-                    def _():
-                        decay_copy(way, d + 1, False).start()
-
-    @scoped
-    def state_hop(d):
-        for half in HALVES:
-            for way in (1, 0):
-                if d and (way, d) in WAYS:
-
-                    @pl.when(hop_valid(way, d, True))
-                    def _():
-                        state_copy(way, d, True, half).wait_recv()
-
-                if (way, d + 1) in WAYS:
-
-                    @pl.when(hop_valid(way, d + 1, False))
-                    def _():
-                        state_copy(way, d + 1, False, half).start()
-
-    def hops_done():
-        for way, d in WAYS:
-
-            @pl.when(hop_valid(way, d, False))
+        @pl.when((c == 1) & ((z == 4 + d) | (z == 3 - d)))
+        def _():
+            onward = remote(
+                decays.at[2], decays.at[1], e_ssem.at[0], e_rsem.at[0], ((z + jnp.where(z >= 4, 1, 7)) & 7, 1, x, y)
+            )
+            if d:
+                onward.wait_recv()
+            else:
+                decays[1] = jnp.ones((1, 512), F32)
+            if d < 3:
+                decays[2] = decays[1] * decays[0]
+                onward.start()
+
+    def down_task(q):
+        piece = QUARTERS[q]
+        leg_wait(X, q)
+        mout[piece, :] = (schip[piece, :] + decays[0] * legs[X, piece, :].astype(F32)).astype(BF16)
+
+        @pl.when(z == 4)
+        def _():
+            leg(mout, R, q, -1).start()
+
+        @pl.when(z != 4)
+        def _():
+            leg(mout, X, q, -1).start()
+
+    def up_task(q):
+        piece = QUARTERS[q]
+        leg_wait(V, q)
+        vout[piece, :] = (legs[V, piece, :].astype(F32) + decays[1] * schip[piece, :]).astype(BF16)
+
+        @pl.when(z == 7)
+        def _():
+            leg(vout, R, q, 1).start()
+
+        @pl.when(z != 7)
+        def _():
+            leg(vout, V, q, 1).start()
+
+    def quarters(when, fn):
+        @pl.when(when)
+        def _():
+            for q in range(4):
+                fn(q)
+
+    @scoped
+    def exchange():
+        for q in range(4):
+            piece = QUARTERS[q]
+
+            @pl.when((z == 7) | (z == 3))
             def _():
-                decay_copy(way, d, False).wait_send()
-                for half in HALVES:
-                    state_copy(way, d, False, half).wait_send()
+                mout[piece, :] = schip[piece, :].astype(BF16)
+                leg(mout, X, q, -1).start()
+
+            @pl.when(z == 4)
+            def _():
+                vout[piece, :] = schip[piece, :].astype(BF16)
+                leg(vout, V, q, 1).start()
+
+    @scoped
+    def exchange_rest():
+        quarters((z == 6) | (z == 2), down_task)
+        quarters(z == 5, up_task)
+        quarters((z == 5) | (z == 1), down_task)
+        quarters(z == 6, up_task)
+        quarters(z == 4, down_task)
+        quarters(z == 7, up_task)
+        quarters(z == 0, lambda q: leg_wait(X, q))
+
+        def pass_on(dz):
+            def fn(q):
+                leg_wait(R, q)
+                leg(legs.at[R], R, q, dz).start()
+
+            return fn
+
+        quarters(z == 3, pass_on(-1))
+        quarters(z == 0, pass_on(1))
+        quarters((z == 2) | (z == 1), lambda q: leg_wait(R, q))
+
+        @pl.when(z == 7)
+        def _():
+            acc[...] = jnp.zeros((128, 512), F32)
+
+        @pl.when((z >= 4) & (z < 7))
+        def _():
+            acc[...] = legs[X].astype(F32)
+
+        @pl.when(z == 3)
+        def _():
+            acc[...] = legs[R].astype(F32)
+
+        @pl.when(z < 3)
+        def _():
+            acc[...] = legs[X].astype(F32) + decays[1] * legs[R].astype(F32)
+
+    def exchange_sent():
+        def sent(kind):
+            pltpu.make_async_copy(legs.at[kind], legs.at[kind], m_ssem.at[kind]).wait()
+
+        @pl.when((z != 0) & (z != 4))
+        def _():
+            sent(X)
+
+        @pl.when((z >= 4) & (z < 7))
+        def _():
+            sent(V)
+
+        @pl.when((z == 4) | (z == 7) | (z == 3) | (z == 0))
+        def _():
+            sent(R)
+
+        @pl.when((z != 7) & (z != 0))
+        def _():
+            pltpu.make_async_copy(decays.at[2], decays.at[2], e_ssem.at[0]).wait()
 
     def s0_copy():
         return remote(s0buf.at[0], s0buf.at[1], s_ssem.at[0], s_rsem.at[0], (z, 1, x, y))
@@ -487,8 +573,8 @@
     a_send(*every(0))
     for k in (0, 1):
         for d in (0, 1):
-            w_copy(d, k, False).start()
-    b_copy(0, False).start()
+            w_copy(d, k).start()
+    b_copy(0).start()
     gate_phase()
     row_send(sqs, g_ssem, g_rsem)
     a_send(*every(1))
@@ -501,7 +587,7 @@
     w_event(0)
     pick_group()
     w_event(1)
-    a_wait(*every(0))
+    a_wait(0)
     a_send((0, 2), (0, 3), (0, 4), (1, 3), (3, 2), (3, 3), (3, 4), (2, 3))
     block_weights()
     w_event(2)
@@ -509,53 +595,52 @@
     @pl.when(c == 1)
     def _():
         d0_copy().wait_recv()
-        dall[z] = d0buf[0] * d0buf[1]
-
-    normalize(row_sum(sqs, g_ssem, g_rsem) * (1.0 / 8192))
+        decays[0] = d0buf[0] * d0buf[1]
+
+    normalize(row_sum(sqs, g_rsem) * (1.0 / 8192))
     w_event(3)
     decay_hop(0)
-    a_wait(*every(1))
+    a_wait(1)
     a_send((1, 2), (1, 4), (2, 2), (2, 4))
-    weight_part(G0)
+    weight_part(G0A)
+    weight_part(G0B)
     w_event(4)
     w_event(5)
+    rs_stage((G0A, 0))
     decay_hop(1)
-    a_wait((0, 2), (3, 2), (1, 3), (2, 3))
+    a_wait(2)
     a_send((2, 5), (3, 5), (1, 6))
-    rs_stage((G0A, 0))
     w_event(6)
+    rs_stage((G0B, 0))
     decay_hop(2)
-    a_wait((0, 3), (1, 2), (2, 2), (3, 3))
+    a_wait(3)
     a_send((0, 6), (2, 6), (3, 6))
-    rs_stage((G0B, 0))
+    rs_stage((G0A, 1))
     weight_part(G1)
     with jax.named_scope("b_wait"):
-        for k in range(8):
-            b_copy(k, True).wait_recv()
+        whole(wbuf, 8, b_rsem.at[0])
     grad_part(range(0, 4))
-    rs_stage((G0A, 1), (G1, 0))
-    a_wait(*every(4))
+    rs_stage((G0B, 1), (G1, 0))
+    decay_hop(3)
+    a_wait(4)
     a_send((0, 7), (1, 7), (2, 7), (3, 7), (0, 5), (1, 5), (0, 9), (1, 9))
     grad_part(range(4, 8))
-    decay_hop(3)
-    rs_stage((G0B, 1))
+    rs_stage((G0A, 2))
     weight_part(G2)
-    rs_stage((G0A, 2))
     grad_part(G2)
-    a_wait((0, 6), (1, 6), (0, 7), (1, 7), (2, 5), (3, 5))
+    rs_stage((G0B, 2), (G1, 1))
+    a_wait(5)
     a_send((2, 8), (3, 8))
-    rs_stage((G1, 1), (G2, 0))
+    rs_stage((G2, 0))
     weight_part(G3)
-    decay_hop(4)
-    rs_stage((G0B, 2))
-    a_wait((0, 5), (1, 5), (2, 6), (3, 6))
+    rs_stage((G0A, 3))
+    a_wait(6)
     a_send((0, 8), (1, 8))
     grad_part(G3)
-    rs_stage((G0A, 3), (G3, 0))
-    a_wait((0, 9), (1, 9), (2, 7), (3, 7))
+    rs_stage((G3, 0))
+    a_wait(7)
     grad_part(range(13, 15))
-    rs_stage((G1, 2), (G2, 1))
-    a_wait(*every(8))
+    a_wait(8)
 
     with jax.named_scope("weighted"):
         last = owners[15]
@@ -569,19 +654,11 @@
             wds[head, :, rows] = jnp.sum(fold_lanes(term).T, axis=0, keepdims=True)
 
     row_send(wds, d_ssem, d_rsem)
+    rs_stage((G0B, 3), (G1, 2), (G2, 1))
     weight_part(G4)
-    rs_stage((G4, 0), (G0B, 3), (G3, 1), (G1, 3), (G2, 2))
-
-    @pl.when(c == 1)
-    def _():
-        weight[1] = jnp.ones((1, 512), F32)
-        for k in range(2, 8):
-
-            @pl.when(z + k <= 7)
-            def _():
-                weight[k] = weight[k - 1] * dall[jnp.minimum(z + k - 1, 7)]
-
-    weighted = row_sum(wds, d_ssem, d_rsem)
+    rs_stage((G4, 0), (G3, 1))
+
+    weighted = row_sum(wds, d_rsem)
 
     gs = gt
     with jax.named_scope("grads"):
@@ -630,46 +707,24 @@
                     odd, jnp.where(low, zero, g), preferred_element_type=F32
                 )
 
-    rs_stage((G4, 1), (G3, 2))
+    rs_stage((G4, 1))
     within_all()
-    rs_stage((G2, 3))
+    rs_stage((G1, 3), (G3, 2), (G2, 2), (G0A, 4))
 
     @pl.when(c == 1)
     def _():
         own = d0buf[1] * summary()
         with jax.named_scope("s0_wait"):
             s0_copy().wait_recv()
-        sall[z] = (s0buf[1].astype(F32) + own).astype(BF16)
-        state_hop(0)
-
-    def take(k):
-        @pl.when(z + k <= 7)
-        def _():
-            acc[...] += weight[k] * sall[jnp.minimum(z + k, 7)].astype(F32)
-
-    def hop_and_take(d):
-        @pl.when(c == 1)
-        def _():
-            state_hop(d)
-            if d == 1:
-                acc[...] = jnp.zeros((128, 512), F32)
-            take(d)
-            if d < 4:
-                take(8 - d)
+        schip[...] = s0buf[1].astype(F32) + own
+        exchange()
 
     with jax.named_scope("sends_1"):
-        for d in range(4):
-            for k in range(len(ITEMS[d])):
-                a_copy(d, k, False).wait_send()
-        for d in (0, 1):
-            for k in range(7):
-                w_copy(d, k, False).wait_send()
-        for k in range(8):
-            b_copy(k, False).wait_send()
-        row_done(sqs, g_ssem, g_rsem)
-        row_done(wds, d_ssem, d_rsem)
-    for d in (1, 2, 3, 4):
-        hop_and_take(d)
+        whole(abuf, 15, a_ssem.at[0])
+        whole(wbuf, 15, w_ssem.at[0])
+        whole(sqs, 15, g_ssem.at[0])
+        whole(wds, 15, d_ssem.at[0])
+    pl.when(c == 1)(exchange_rest)
 
     @pl.when(c == 1)
     def _():
@@ -677,7 +732,7 @@
         carry[0] = (own + d0buf[0] * acc[...]).astype(BF16)
         core_copy().start()
 
-    rs_stage((G4, 2), (G3, 3), (G0A, 4), (G0B, 4))
+    rs_stage((G4, 2), (G2, 3), (G3, 3), (G0B, 4))
     rs_stage((G4, 3), (G1, 4), (G2, 4), (G3, 4), (G4, 4))
 
     @pl.when((c == 0) & handed)
@@ -709,13 +764,13 @@
             x_out.start()
             x_outs.append(x_out)
 
-    @pl.when((c == 1) & handed)
+    gw_out = pltpu.make_async_copy(gw.at[c], gw_hbm, l_sem.at[1])
+    own_rows = (c == 0) | jnp.logical_not(handed)
+
+    @pl.when(own_rows)
     def _():
-        with jax.named_scope("out_wait"):
-            out_copy().wait_recv()
-
-    gw_out = pltpu.make_async_copy(gw.at[c], gw_hbm, l_sem.at[1])
-    gw_out.start()
+        gw_out.start()
+
 
     with jax.named_scope("sends_2"):
 
@@ -731,23 +786,23 @@
         @pl.when(c == 1)
         def _():
             core_copy().wait_send()
-            hops_done()
+            exchange_sent()
 
         for q in range(16):
 
-            @pl.when(given(q))
+            @pl.when(given(q) | (((z - (owners[q] >> 1) + 8) & 7) != 0))
             def _():
                 give_copy(q).wait_send()
 
-            @pl.when(kept(q) & (((z - (owners[q] >> 1) + 8) & 7) != 0))
-            def _():
-                for i in (0, 1):
-
-                    @functools.partial(cuts, q)
-                    def _(n):
-                        r_copy(q, i, n, 0).wait_send()
-
-        gw_out.wait()
+        @pl.when((c == 1) & handed)
+        def _():
+            with jax.named_scope("out_wait"):
+                out_copy().wait_recv()
+
+        @pl.when(own_rows)
+        def _():
+            gw_out.wait()
+
         for x_out in x_outs:
             x_out.wait()
 
@@ -762,7 +817,7 @@
             steps.append(
                 (
                     pltpu.make_async_copy(ins[k].at[rows], bufs[k].at[rows], in_sem.at[k, r]),
-                    pltpu.make_async_copy(bufs[k].at[rows], outs[k].at[rows], out_sem.at[k, r]),
+                    pltpu.make_async_copy(bufs[k].at[rows], outs[k].at[rows], out_sem.at[k]),
                 )
             )
     for first, _ in steps:
@@ -770,8 +825,8 @@
     for first, second in steps:
         first.wait()
         second.start()
-    for _, second in steps:
-        second.wait()
+    for k in range(3):
+        pltpu.make_async_copy(bufs[k], outs[k], out_sem.at[k]).wait()
 
 
 def on_device(a, w, so, gt, nw, ts, ld, bin_, cin, skip):
@@ -796,11 +851,11 @@
             V((512, 1024), BF16), V((2048, 128), F32), V((1024, 128), BF16),
             V((1024, 128), BF16), V((128, 1024), BF16), V((1024, 128), F32), V((8, 1024), F32), V((1024, 128), F32),
             V((16, 1, 1024), F32), V((16, 1, 1024), F32), V((4, 128, 512), F32), V((128, 512), F32),
-            V((2, 128, 512), BF16), V((2, 1, 512), F32), V((8, 128, 512), BF16), V((8, 1, 512), F32),
-            V((8, 1, 512), F32), V((2, 128, 512), BF16), V((2, 256, 512), F32),
-            D((4, 10)), D((4, 10)), D((2, 7)), D((2, 7)), D((8,)), D((8,)), D((16, 2, 4)), D((16, 2, 2, 4)), D((16,)), D((16,)),
-            D((16,)), D((16,)), D((16,)), D((16,)), D((2,)), D((2,)), D((1,)), D((1,)), D((2, 4, 8)), D((2, 4, 8)),
-            D((2, 4)), D((2, 4)), D((1,)), D((1,)), D((6,)),
+            V((2, 128, 512), BF16), V((2, 1, 512), F32), V((128, 512), F32),
+            V((3, 128, 512), BF16), V((128, 512), BF16), V((128, 512), BF16), V((3, 1, 512), F32), V((2, 128, 512), BF16), V((2, 256, 512), F32),
+            D((1,)), D((9,)), D((1,)), D((7,)), D((1,)), D((16,)), D((50,)), D((1,)), D((1,)), D((16,)),
+            D((1,)), D((1,)), D((2,)), D((2,)), D((1,)), D((1,)), D((3,)), D((3, 4)), D((1,)), D((1,)), D((1,)), D((3,)),
+            D((6,)),
         ],
         compiler_params=pltpu.CompilerParams(
             collective_id=0, has_side_effects=True, vmem_limit_bytes=59768832
@@ -815,7 +870,7 @@
         out_shape=[jax.ShapeDtypeStruct(r.shape, r.dtype) for r in results],
         in_specs=[any_] * 3,
         out_specs=[any_] * 3,
-        scratch_shapes=[V(r.shape, r.dtype) for r in results] + [D((3, 4)), D((3, 4))],
+        scratch_shapes=[V(r.shape, r.dtype) for r in results] + [D((3, 4)), D((3,))],
         compiler_params=pltpu.CompilerParams(vmem_limit_bytes=62914560),
         name="move",
     )(*results)

time: 91.8 us -> 85.5 us (0.931)
  the two profiles are of different devices: /device:TPU:21 before, /device:TPU:64 now
where the time goes in v4:
time: 85.5 us; the launch traced here: 85.4 us
  Pallas kernels  84.7 us (99%)
    pallas_call x1, Pallas kernels, on_device(): pl.pallas_call(kernel, out_shape=(jax.ShapeDtypeStruct((1024, 512), BF16)...  82.2 us
    pallas_call x1, Pallas kernels, on_device(): pl.pallas_call(move, out_shape=[jax.ShapeDtypeStruct(r.shape, r.dtype) fo...  2.55 us

profile of v4, /device:TPU:64, one launch (start us, length us, event | category | flops | bytes accessed | tf_op | source)
XLA Modules:
  0.0 85.4 jit_solution(11278632252069775158)
XLA Ops:
  0.6 82.2 %mixer_backward.1 = (bf16[1024,512]{1,0:T(8,128)(2,1)}, bf16[1024,512]{1,0:T(8,128)(2,1)}, f32[256,512]{1,0:T(8,128)}) custom-call(bf16[1024,256]{1,0:T(8,128)(2,1)} %a_hbm.1, bf16[256,512]{1,0:T(8,128)(2,1)} %w_hbm.1, bf16[1024,512]{1,0:T(8,128)(2,1)} %so_hbm.1, bf16[1024,512]{1,0:T(8,128)(2,1)} %gt_hbm.1, f32[1,512]{1,0:T(1,128)} %bitcast.6, ...), custom_call_target="tpu_custom_call" | custom-call | tf_op jit(solution)/shard_map/mixer_backward/pallas_call | solution.py:837
  82.8 2.6 %move.1 = (bf16[1024,512]{1,0:T(8,128)(2,1)}, bf16[1024,512]{1,0:T(8,128)(2,1)}, f32[256,512]{1,0:T(8,128)}) custom-call(bf16[1024,512]{1,0:T(8,128)(2,1)} %get-tuple-element.6.refs_0_, bf16[1024,512]{1,0:T(8,128)(2,1)} %get-tuple-element.7.refs_1_, f32[256,512]{1,0:T(8,128)} %get-tuple-element.8.refs_2_), custom_call_target="tpu_custom_call" | custom-call | tf_op jit(solution)/shard_map/move/pallas_call | solution.py:868
